TPU v7x, 32 devices: a whole 2x2x4 slice. The times are simulated.
32 devices in a mesh: dp: 4 (over y, x), head: 4 (over z), ctx: 2 (over core).
Axes of the slice: x: 2, y: 2, z: 4, core: 2. Of those that a mesh axis runs over, the one named last changes fastest.
Arguments:
- tokens: bfloat16 [8192, 768], P(('dp', 'head', 'ctx')), may hold values from -6 to 6
- cotangent: bfloat16 [8192, 768], P(('dp', 'head', 'ctx')), may hold values from -6 to 6
- in_master: float32 [768, 3968], P('head'), may hold values from -4 to 4
- in_moment: float32 [768, 3968], P('head'), may hold values from -245760 to 245760
- in_second: float32 [768, 3968], P('head'), may hold values from 0 to 8192000, as said below
- out_master: float32 [3840, 768], P('head'), may hold values from -4 to 4
- out_moment: float32 [3840, 768], P('head'), may hold values from -245760 to 245760
- out_second: float32 [3840, 768], P('head'), may hold values from 0 to 8192000, as said below
- vec_master: float32 [7808], replicated, may hold values from -4 to 4
- vec_moment: float32 [7808], replicated, may hold values from -245760 to 245760
- vec_second: float32 [7808], replicated, may hold values from 0 to 8192000, as said below
- rotary_scale: int32 [1], replicated, may hold values from 2 to 8
Outputs:
- output: bfloat16 [8192, 768], P(('dp', 'head', 'ctx'))
- input_grad: bfloat16 [8192, 768], P(('dp', 'head', 'ctx'))
- in_moment_new: float32 [768, 3968], P('head')
- in_second_new: float32 [768, 3968], P('head')
- in_master_new: float32 [768, 3968], P('head')
- in_copy: bfloat16 [768, 3968], P('head')
- out_moment_new: float32 [3840, 768], P('head')
- out_second_new: float32 [3840, 768], P('head')
- out_master_new: float32 [3840, 768], P('head')
- out_copy: bfloat16 [3840, 768], P('head')
- vec_moment_new: float32 [7808], replicated
- vec_second_new: float32 [7808], replicated
- vec_master_new: float32 [7808], replicated
Inputs may be any that keep to these rules, and one draw needn't show every extreme that they name: `in_second`: positive entries. `out_second`: positive entries. `vec_second`: positive entries.
All inputs are finite; a program needn't handle non-finite values.
Results may differ from a plain program's by a relative error of at most 0.014.
The roundings to bfloat16 on the way count: a program that leaves them out, or rounds other values in their place, can miss the bound.
Values may be sent and summed in bfloat16 or wider, within the bound.
A program may use at most 192 MiB of HBM per device.

v0:
```python
import jax
import jax.numpy as jnp
from jax import lax
from jax.experimental import pallas as pl
from jax.experimental.pallas import tpu as pltpu
from jax.sharding import PartitionSpec as P

HEADS = 12
HEAD_DIM = 64
ROT = 16
D = 768
KEY_BLOCK = 1024
ADAM_STEP = 3


neg_fill = -1e30
matrix_rate = 0.03
vector_rate = 0.3
weight_decay = 0.1
adam_epsilon = 1e-08
contract_rows = (((0,), (0,)), ((), ()))
contract_cols = (((1,), (1,)), ((), ()))


def layer_norm(values, norm_gain, norm_shift):
    center = values - jnp.mean(values, axis=-1, keepdims=True)
    inverse = lax.rsqrt(jnp.mean(center * center, axis=-1, keepdims=True) + 1e-05)
    normed = center * inverse
    return (normed * norm_gain + norm_shift, normed, inverse)


def norm_back(upstream, normed, inverse, norm_gain):
    scaled = upstream * norm_gain
    inside = (
        scaled
        - jnp.mean(scaled, axis=-1, keepdims=True)
        - normed * jnp.mean(scaled * normed, axis=-1, keepdims=True)
    )
    return (inverse * inside, jnp.sum(upstream * normed, axis=0), jnp.sum(upstream, axis=0))


def rotary_tables(positions, scale_value):
    half_rot = ROT // 2
    frequency = 10000.0 ** (-(2.0 * jnp.arange(half_rot, dtype=jnp.float32)) / ROT)
    angles = (positions / scale_value)[:, None] * frequency[None, :]
    return (jnp.cos(angles), jnp.sin(angles))


def rotate(values, cosine, sine_table):
    half_rot = ROT // 2
    front_half = values[..., :half_rot]
    back_half = values[..., half_rot:ROT]
    return jnp.concatenate(
        [
            front_half * cosine - back_half * sine_table,
            back_half * cosine + front_half * sine_table,
            values[..., ROT:],
        ],
        axis=-1,
    )


def score_block(query_rows, row_pos, whole_kv, block_index):
    key_block = lax.dynamic_slice_in_dim(whole_kv, block_index * KEY_BLOCK, KEY_BLOCK, 0)
    scores = lax.dot_general(
        query_rows, key_block[:, :HEAD_DIM], contract_cols, preferred_element_type=jnp.float32
    )
    key_pos = block_index * KEY_BLOCK + jnp.arange(KEY_BLOCK, dtype=jnp.int32)
    allowed = key_pos[None, :] <= row_pos[:, None]
    return (jnp.where(allowed, scores, neg_fill), allowed, key_block)


def log_totals(query_rows, row_pos, whole_kv):
    row_count = query_rows.shape[0]
    last_pos = jnp.max(row_pos)

    def advance(block_index, state_now):

        def process(state_old):
            run_max, run_sum = state_old
            scores, allowed, key_block = score_block(query_rows, row_pos, whole_kv, block_index)
            new_max = jnp.maximum(run_max, jnp.max(scores, axis=1))
            weights = jnp.where(allowed, jnp.exp(scores - new_max[:, None]), 0.0)
            return (new_max, run_sum * jnp.exp(run_max - new_max) + jnp.sum(weights, axis=1))

        return lax.cond(
            block_index * KEY_BLOCK <= last_pos, process, lambda state_same: state_same, state_now
        )

    start_state = (
        jnp.full((row_count,), neg_fill, jnp.float32),
        jnp.zeros((row_count,), jnp.float32),
    )
    run_max, run_sum = lax.fori_loop(0, whole_kv.shape[0] // KEY_BLOCK, advance, start_state)
    return run_max + jnp.log(run_sum)


def attend(query_rows, row_pos, whole_kv, log_sum):
    last_pos = jnp.max(row_pos)

    def advance(block_index, summed):

        def process(summed_old):
            scores, allowed, key_block = score_block(query_rows, row_pos, whole_kv, block_index)
            probs = jnp.where(allowed, jnp.exp(scores - log_sum[:, None]), 0.0).astype(jnp.bfloat16)
            return summed_old + jnp.dot(
                probs, key_block[:, HEAD_DIM:], preferred_element_type=jnp.float32
            )

        return lax.cond(
            block_index * KEY_BLOCK <= last_pos, process, lambda summed_same: summed_same, summed
        )

    start_state = jnp.zeros((query_rows.shape[0], HEAD_DIM), jnp.float32)
    return lax.fori_loop(0, whole_kv.shape[0] // KEY_BLOCK, advance, start_state)


def attend_back(query_rows, row_pos, whole_kv, log_sum, grad_rows, row_inner):
    last_pos = jnp.max(row_pos)

    def advance(block_index, state_now):

        def process(state_old):
            query_grad, kv_terms = state_old
            scores, allowed, key_block = score_block(query_rows, row_pos, whole_kv, block_index)
            probs = jnp.where(allowed, jnp.exp(scores - log_sum[:, None]), 0.0)
            prob_grad = lax.dot_general(
                grad_rows,
                key_block[:, HEAD_DIM:],
                contract_cols,
                preferred_element_type=jnp.float32,
            )
            score_grad = (probs * (prob_grad - row_inner[:, None])).astype(jnp.bfloat16)
            query_grad = query_grad + jnp.dot(
                score_grad, key_block[:, :HEAD_DIM], preferred_element_type=jnp.float32
            )
            key_grad = lax.dot_general(
                score_grad, query_rows, contract_rows, preferred_element_type=jnp.float32
            )
            value_grad = lax.dot_general(
                probs.astype(jnp.bfloat16),
                grad_rows,
                contract_rows,
                preferred_element_type=jnp.float32,
            )
            kv_terms = lax.dynamic_update_slice_in_dim(
                kv_terms,
                jnp.concatenate([key_grad, value_grad], axis=1),
                block_index * KEY_BLOCK,
                0,
            )
            return (query_grad, kv_terms)

        return lax.cond(
            block_index * KEY_BLOCK <= last_pos, process, lambda state_same: state_same, state_now
        )

    start_state = (
        jnp.zeros((query_rows.shape[0], HEAD_DIM), jnp.float32),
        jnp.zeros((whole_kv.shape[0], 2 * HEAD_DIM), jnp.float32),
    )
    return lax.fori_loop(0, whole_kv.shape[0] // KEY_BLOCK, advance, start_state)


def adam_update(master, moment, second, gradient, step_rate, decay_rate):
    moment_new = 0.5 * moment + 0.5 * gradient
    second_new = 0.5 * second + 0.5 * gradient * gradient
    correction = 1.0 - 0.5**ADAM_STEP
    normalized = moment_new / correction / (jnp.sqrt(second_new / correction) + adam_epsilon)
    return (moment_new, second_new, master - step_rate * (normalized + decay_rate * master))


def shards(
    tokens,
    cotangent,
    in_master,
    in_moment,
    in_second,
    out_master,
    out_moment,
    out_second,
    vec_master,
    vec_moment,
    vec_second,
    rotary_scale,
):
    local_rows = tokens.shape[0]
    full_in, full_out = (
        lax.all_gather(in_master.astype(jnp.bfloat16), "head", axis=0, tiled=True),
        lax.all_gather(out_master.astype(jnp.bfloat16), "head", axis=0, tiled=True),
    )
    scale_value = rotary_scale[0].astype(jnp.float32)
    local_pos = lax.axis_index(("head", "ctx")) * local_rows + jnp.arange(
        local_rows, dtype=jnp.int32
    )
    cosine, sine_table = rotary_tables(local_pos.astype(jnp.float32), scale_value)
    inputs = tokens.astype(jnp.float32)
    norm_one, normed_one, inverse_one = layer_norm(inputs, vec_master[0:D], vec_master[D : 2 * D])
    norm_two, normed_two, inverse_two = layer_norm(
        inputs, vec_master[2 * D : 3 * D], vec_master[3 * D : 4 * D]
    )
    first_in = norm_one.astype(jnp.bfloat16)
    second_in = norm_two.astype(jnp.bfloat16)
    projected = (
        jnp.dot(first_in, full_in[:, : D + 2 * HEAD_DIM], preferred_element_type=jnp.float32)
        + vec_master[5 * D : 6 * D + 2 * HEAD_DIM]
    )
    hidden_in = (
        jnp.dot(second_in, full_in[:, D + 2 * HEAD_DIM :], preferred_element_type=jnp.float32)
        + vec_master[6 * D + 2 * HEAD_DIM :]
    )
    query_heads = projected[:, :D].reshape(local_rows, HEADS, HEAD_DIM)
    queries = (
        (rotate(query_heads, cosine[:, None, :], sine_table[:, None, :]) * 0.125)
        .astype(jnp.bfloat16)
        .reshape(local_rows, D)
    )
    key_part = rotate(projected[:, D : D + HEAD_DIM], cosine, sine_table)
    shared = jnp.concatenate([key_part, projected[:, D + HEAD_DIM :]], axis=1).astype(jnp.bfloat16)
    whole_kv = lax.all_gather(shared, ("head", "ctx"), axis=0, tiled=True)
    activated = jax.nn.gelu(hidden_in, approximate=False).astype(jnp.bfloat16)
    heads_here = queries.shape[1] // HEAD_DIM
    query_rows = queries.reshape(-1, HEAD_DIM)
    row_pos = jnp.repeat(local_pos, heads_here)
    log_sum = log_totals(query_rows, row_pos, whole_kv)
    attended = attend(query_rows, row_pos, whole_kv, log_sum)
    att_out = attended.reshape(queries.shape).astype(jnp.bfloat16)
    branch_pair = jnp.concatenate([att_out, activated], axis=1)
    output = (
        inputs
        + jnp.dot(branch_pair, full_out, preferred_element_type=jnp.float32)
        + vec_master[4 * D : 5 * D]
    ).astype(jnp.bfloat16)
    cot_in = cotangent.astype(jnp.float32)
    grad_out = lax.dot_general(
        branch_pair, cotangent, contract_rows, preferred_element_type=jnp.float32
    )
    back_proj = lax.dot_general(
        cotangent, full_out, contract_cols, preferred_element_type=jnp.float32
    )
    branch_grad = back_proj[:, :D].astype(jnp.bfloat16)
    gelu_back = jax.vjp(lambda pre_act: jax.nn.gelu(pre_act, approximate=False), hidden_in)[1]
    hidden_grad = gelu_back(back_proj[:, D:])[0].astype(jnp.bfloat16)
    grad_rows = branch_grad.reshape(-1, HEAD_DIM)
    row_inner = jnp.sum(grad_rows.astype(jnp.float32) * attended, axis=1)
    query_grad, kv_terms = attend_back(query_rows, row_pos, whole_kv, log_sum, grad_rows, row_inner)
    att_cos, att_sin = rotary_tables(local_pos.astype(jnp.float32), scale_value)
    query_pre = rotate(
        query_grad.reshape(-1, heads_here, HEAD_DIM) * 0.125,
        att_cos[:, None, :],
        -att_sin[:, None, :],
    )
    query_pre = query_pre.reshape(queries.shape).astype(jnp.bfloat16)
    kv_sum = lax.psum_scatter(kv_terms, ("head", "ctx"), scatter_dimension=0, tiled=True)
    shared_grad = jnp.concatenate(
        [rotate(kv_sum[:, :HEAD_DIM], cosine, -sine_table), kv_sum[:, HEAD_DIM:]], axis=1
    ).astype(jnp.bfloat16)
    attn_grad = jnp.concatenate([query_pre, shared_grad], axis=1)
    grad_in = jnp.concatenate(
        [
            lax.dot_general(first_in, attn_grad, contract_rows, preferred_element_type=jnp.float32),
            lax.dot_general(
                second_in, hidden_grad, contract_rows, preferred_element_type=jnp.float32
            ),
        ],
        axis=1,
    )
    norm_grad_one = lax.dot_general(
        attn_grad, full_in[:, : D + 2 * HEAD_DIM], contract_cols, preferred_element_type=jnp.float32
    )
    norm_grad_two = lax.dot_general(
        hidden_grad,
        full_in[:, D + 2 * HEAD_DIM :],
        contract_cols,
        preferred_element_type=jnp.float32,
    )
    input_one, gain_one, shift_one = norm_back(
        norm_grad_one, normed_one, inverse_one, vec_master[0:D]
    )
    input_two, gain_two, shift_two = norm_back(
        norm_grad_two, normed_two, inverse_two, vec_master[2 * D : 3 * D]
    )
    input_grad = (cot_in + input_one + input_two).astype(jnp.bfloat16)
    grad_vec = jnp.concatenate(
        [
            gain_one,
            shift_one,
            gain_two,
            shift_two,
            jnp.sum(cot_in, axis=0),
            jnp.sum(attn_grad.astype(jnp.float32), axis=0),
            jnp.sum(hidden_grad.astype(jnp.float32), axis=0),
        ]
    )
    shard_in, shard_out = (
        lax.psum_scatter(
            grad_in.astype(jnp.bfloat16), "head", scatter_dimension=0, tiled=True
        ).astype(jnp.float32),
        lax.psum_scatter(
            grad_out.astype(jnp.bfloat16), "head", scatter_dimension=0, tiled=True
        ).astype(jnp.float32),
    )
    summed_in, summed_out = lax.psum((shard_in, shard_out), ("dp", "ctx"))
    summed_vec = lax.psum(grad_vec, ("dp", "head", "ctx"))
    in_moment_new, in_second_new, in_master_new = adam_update(
        in_master, in_moment, in_second, summed_in, matrix_rate, weight_decay
    )
    out_moment_new, out_second_new, out_master_new = adam_update(
        out_master, out_moment, out_second, summed_out, matrix_rate, weight_decay
    )
    vec_moment_new, vec_second_new, vec_master_new = adam_update(
        vec_master, vec_moment, vec_second, summed_vec, vector_rate, 0.0
    )
    return (
        output,
        input_grad,
        in_moment_new,
        in_second_new,
        in_master_new,
        in_master_new.astype(jnp.bfloat16),
        out_moment_new,
        out_second_new,
        out_master_new,
        out_master_new.astype(jnp.bfloat16),
        vec_moment_new,
        vec_second_new,
        vec_master_new,
    )


MESH = pl.DeviceIdType.MESH
F32 = jnp.float32
BF16 = jnp.bfloat16
HALF_HEADS = HEADS // 2
VMEM_LIMIT = 60 * 1024 * 1024
BACK_LIMIT = 67000000


def vmem_specs(count):
    return [pl.BlockSpec(memory_space=pltpu.VMEM)] * count


def places():
    z = lax.axis_index("head")
    q = lax.axis_index("dp")
    c = lax.axis_index("ctx")
    qx = lax.rem(q, 2)
    qy = q // 2
    return z, q, c, qx, qy, qy * 2 + 1 - qx, (1 - qy) * 2 + qx


def greet(partners):
    barrier = pltpu.get_barrier_semaphore()
    for partner in partners:
        pl.semaphore_signal(barrier, inc=1, device_id=partner, device_id_type=MESH)
    pl.semaphore_wait(barrier, len(partners))


def remote(source, target, send_sem, recv_sem, device):
    return pltpu.make_async_remote_copy(
        src_ref=source,
        dst_ref=target,
        send_sem=send_sem,
        recv_sem=recv_sem,
        device_id=device,
        device_id_type=MESH,
    )


CHUNK = 512
IN_ROWS = 48
OUT_ROWS = 120


def front_kernel(
    win,
    wout,
    tok,
    cot,
    affine,
    bias,
    cos_ref,
    sin_ref,
    full_in,
    full_out,
    all_tok,
    all_cot,
    norm_one,
    norm_two,
    att_ref,
    dq_ref,
    dkv_ref,
    q_all,
    g_all,
    kv_all,
    keys,
    values,
    weights,
    tops,
    dkeys,
    dvalues,
    z_send,
    z_recv,
    xy_send,
    xy_recv,
    pair_send,
    pair_recv,
    kv_send,
    kv_recv,
    local_sem,
):
    z, q, c, qx, qy, xn, yn = places()
    dg = (1 - qy) * 2 + 1 - qx
    to_x, to_y, to_pair = (xn, z, c), (yn, z, c), (q, z, 1 - c)
    greet([(q, lax.rem(z + k, 4), c) for k in (1, 2, 3)] + [to_x, to_y, to_pair])
    attn_cols = HALF_D + 2 * HEAD_DIM
    groups = ((0, 0, attn_cols), (1, 0, D), (0, attn_cols, win.shape[1]))
    own = (win, wout)
    full = (full_in, full_out)
    piece_rows = (IN_ROWS, OUT_ROWS)

    def span(group, part):
        which, first, last = groups[group]
        middle = (first + last) // 2
        if part == 1:
            return which, pl.ds(first, middle - first)
        if part == 2:
            return which, pl.ds(middle, last - middle)
        return which, pl.ds(first, last - first)

    def rows_of(which, plane, quarter):
        size = piece_rows[which]
        return pl.ds(pl.multiple_of((plane * 4 + quarter) * size, 8), size)

    def place(group, part, plane, quarter):
        which, cols = span(group, part)
        return full[which].at[rows_of(which, plane, quarter), cols]

    def z_copy(group, k):
        which, cols = span(group, 0)
        return remote(
            own[which].at[rows_of(which, 0, q), cols],
            place(group, 0, z, q),
            z_send.at[group, k],
            z_recv.at[group, z],
            (q, lax.rem(z + k, 4), c),
        )

    def pair_copy(number):
        source, target = ((tok, all_tok), (cot, all_cot))[number]
        return remote(source, target.at[c], pair_send.at[number], pair_recv.at[number], to_pair)

    for number in range(2):
        pair_copy(number).start()
    for group in range(3):
        for k in (1, 2, 3):
            z_copy(group, k).start()

    locals_ = []
    for number, (source, target) in enumerate(
        (
            (win, full_in.at[pl.ds(pl.multiple_of(z * 4 * IN_ROWS, 8), 4 * IN_ROWS), :]),
            (wout, full_out.at[pl.ds(pl.multiple_of(z * 4 * OUT_ROWS, 8), 4 * OUT_ROWS), :]),
            (tok, all_tok.at[c]),
            (cot, all_cot.at[c]),
        )
    ):
        copy = pltpu.make_async_copy(source, target, local_sem.at[number])
        copy.start()
        locals_.append(copy)

    def xy_copy(path, group, plane):
        quarter = (q, q, xn, yn)[path]
        piece = place(group, (0, 0, 1, 2)[path], plane, quarter)
        return remote(
            piece,
            piece,
            xy_send.at[path, group, plane],
            xy_recv.at[path, group, plane],
            (to_x, to_y, to_y, to_x)[path],
        )

    def xy_landed(path, group, plane):
        quarter = (xn, yn, dg, dg)[path]
        piece = place(group, (0, 0, 1, 2)[path], plane, quarter)
        remote(
            piece, piece, xy_send.at[path, group, plane], xy_recv.at[path, group, plane], to_pair
        ).wait_recv()

    def spread(group, plane):
        @pl.when(z != plane)
        def _():
            piece = place(group, 0, plane, q)
            remote(piece, piece, z_send.at[group, 1], z_recv.at[group, plane], to_pair).wait_recv()
            xy_copy(0, group, plane).start()
            xy_copy(1, group, plane).start()

    def relay(group, plane):
        @pl.when(z != plane)
        def _():
            xy_landed(0, group, plane)
            xy_copy(2, group, plane).start()
            xy_landed(1, group, plane)
            xy_copy(3, group, plane).start()

    def settle(group, plane):
        @pl.when(z != plane)
        def _():
            xy_landed(2, group, plane)
            xy_landed(3, group, plane)

    locals_[2].wait()
    locals_[3].wait()
    for number, target in enumerate((all_tok, all_cot)):
        piece = target.at[1 - c]
        remote(piece, piece, pair_send.at[number], pair_recv.at[number], to_pair).wait_recv()
    rows = tok.shape[0]
    for half in range(2):
        inputs = all_tok[half].astype(F32)
        center = inputs - jnp.mean(inputs, axis=-1, keepdims=True)
        inverse = lax.rsqrt(jnp.mean(center * center, axis=-1, keepdims=True) + 1e-05)
        normed = center * inverse
        norm_one[pl.ds(half * rows, rows), :] = (normed * affine[0:1, :] + affine[1:2, :]).astype(BF16)
        norm_two[pl.ds(half * rows, rows), :] = (normed * affine[2:3, :] + affine[3:4, :]).astype(BF16)
    for plane in range(4):
        spread(0, plane)
    for plane in range(4):
        relay(0, plane)
    for plane in range(4):
        settle(0, plane)
    locals_[0].wait()
    locals_[1].wait()

    half_rot = ROT // 2
    cosine, sine = cos_ref[...], sin_ref[...]

    def turn(block, cosine, sine):
        front, back = block[:half_rot], block[half_rot:ROT]
        return jnp.concatenate(
            [front * cosine - back * sine, back * cosine + front * sine, block[ROT:]], axis=0
        )

    projected = (
        jnp.dot(norm_one[...], full_in[:, :attn_cols], preferred_element_type=F32) + bias[...]
    ).T
    key_t = turn(projected[HALF_D : HALF_D + HEAD_DIM], cosine, sine)
    kv_all[z] = jnp.concatenate([key_t, projected[HALF_D + HEAD_DIM :]], axis=0).astype(BF16)

    def kv_copy(k):
        return remote(
            kv_all.at[z], kv_all.at[z], kv_send.at[0, k], kv_recv.at[0, k], (q, lax.rem(z + k, 4), c)
        )

    for k in (1, 2, 3):

        @pl.when(z + k < 4)
        def _():
            kv_copy(k).start()

    for head in range(HALF_HEADS):
        block = turn(projected[head * HEAD_DIM : (head + 1) * HEAD_DIM], cosine, sine) * 0.125
        q_all[:, head * CHUNK : (head + 1) * CHUNK] = block.astype(BF16)
    spread(1, 0)
    dkeys[...] = jnp.zeros_like(dkeys)
    dvalues[...] = jnp.zeros_like(dvalues)

    def spread_block(index):
        place_rows = pl.ds(pl.multiple_of(index * CHUNK, CHUNK), CHUNK)
        turned = kv_all[index].astype(F32).T.astype(BF16)
        keys[place_rows, :] = turned[:, :HEAD_DIM]
        values[place_rows, :] = turned[:, HEAD_DIM:]

    spread_block(z)
    relay(1, 0)
    for k in (1, 2, 3):

        @pl.when(z - k >= 0)
        def _():
            source = lax.rem(z + 4 - k, 4)
            remote(
                kv_all.at[source], kv_all.at[source], kv_send.at[0, k], kv_recv.at[0, k], to_pair
            ).wait_recv()
            spread_block(source)

    settle(1, 0)
    grads_t = jnp.concatenate(
        [
            lax.dot_general(
                full_out[:HALF_D, :], all_cot[half], contract_cols, preferred_element_type=F32
            )
            for half in range(2)
        ],
        axis=1,
    ).astype(BF16)
    for head in range(HALF_HEADS):
        g_all[:, head * CHUNK : (head + 1) * CHUNK] = grads_t[head * HEAD_DIM : (head + 1) * HEAD_DIM]

    width = 2 * CHUNK
    cos_two = jnp.concatenate([cosine, cosine], axis=1)
    sin_two = jnp.concatenate([sine, sine], axis=1)
    polls = (
        ((spread, 1, 1), (spread, 1, 2)),
        ((relay, 1, 1), (relay, 1, 2), (spread, 1, 3)),
        ((relay, 1, 3), (spread, 2, 0)),
        ((relay, 2, 0), (spread, 2, 1), (spread, 2, 2)),
        ((relay, 2, 1), (relay, 2, 2), (spread, 2, 3)),
        ((relay, 2, 3),),
    )

    def poll(pair, late):
        for number in range(3):

            @pl.when(pair == number)
            def _():
                for action, group, plane in polls[2 * number + late]:
                    action(group, plane)

    def two_heads(pair, carry):
        cols = pl.ds(pl.multiple_of(pair * width, width), width)
        queries = q_all[:, cols]
        grads = g_all[:, cols].astype(F32)

        def rows_at(index):
            return pl.ds(pl.multiple_of(index * CHUNK, CHUNK), CHUNK)

        def forward(index, state, diagonal):
            top, total, out = state
            part = jnp.dot(keys[rows_at(index), :], queries, preferred_element_type=F32)
            if diagonal:
                key_place = lax.broadcasted_iota(jnp.int32, (CHUNK, width), 0)
                row_place = lax.rem(lax.broadcasted_iota(jnp.int32, (CHUNK, width), 1), CHUNK)
                part = jnp.where(key_place > row_place, neg_fill, part)
            above = jnp.maximum(top, jnp.max(part, axis=0, keepdims=True))
            part = jnp.exp(part - above)
            rounded = part.astype(BF16)
            weights[rows_at(index), :] = rounded
            tops[index] = above
            scale = jnp.exp(top - above)
            total = total * scale + jnp.sum(part, axis=0, keepdims=True)
            out = out * scale + jnp.dot(
                kv_all[index, HEAD_DIM:, :], rounded, preferred_element_type=F32
            )
            return above, total, out

        state = (
            jnp.full((1, width), neg_fill, F32),
            jnp.zeros((1, width), F32),
            jnp.zeros((HEAD_DIM, width), F32),
        )
        state = lax.fori_loop(0, z, lambda index, state: forward(index, state, False), state)
        top, total, out = forward(z, state, True)
        inverse = 1.0 / total
        out = out * inverse
        base = pl.multiple_of(pair * 2 * HEAD_DIM, 2 * HEAD_DIM)
        second = pl.multiple_of(base + HEAD_DIM, HEAD_DIM)
        att_ref[pl.ds(base, HEAD_DIM), :] = out[:, :CHUNK].astype(BF16)
        att_ref[pl.ds(second, HEAD_DIM), :] = out[:, CHUNK:].astype(BF16)
        inner = jnp.sum(grads * out, axis=0, keepdims=True)
        poll(pair, 0)

        def backward(index, dq):
            here = rows_at(index)
            factor = inverse * jnp.exp(tops[index] - top)
            scaled = (grads * factor).astype(BF16)
            dprob = jnp.dot(values[here, :], scaled, preferred_element_type=F32)
            rounded = weights[here, :]
            dscore = (rounded.astype(F32) * (dprob - inner * factor)).astype(BF16)
            dkeys[here, :] += lax.dot_general(
                dscore, queries, contract_cols, preferred_element_type=F32
            )
            dvalues[here, :] += lax.dot_general(
                rounded, scaled, contract_cols, preferred_element_type=F32
            )
            return dq + jnp.dot(kv_all[index, :HEAD_DIM, :], dscore, preferred_element_type=F32)

        dq = lax.fori_loop(0, z + 1, backward, jnp.zeros((HEAD_DIM, width), F32))
        dq = turn(dq * 0.125, cos_two, -sin_two)
        dq_ref[pl.ds(base, HEAD_DIM), :] = dq[:, :CHUNK].astype(BF16)
        dq_ref[pl.ds(second, HEAD_DIM), :] = dq[:, CHUNK:].astype(BF16)
        poll(pair, 1)
        return carry

    lax.fori_loop(0, HALF_HEADS // 2, two_heads, 0)

    for index in range(4):
        here = pl.ds(index * CHUNK, CHUNK)
        dkv_ref[index] = jnp.concatenate([dkeys[here, :], dvalues[here, :]], axis=1)
    for group, plane in ((1, 1), (1, 2), (1, 3), (2, 0), (2, 1), (2, 2), (2, 3)):
        settle(group, plane)
    for number in range(2):
        pair_copy(number).wait_send()
    for k in (1, 2, 3):
        for group in range(3):
            z_copy(group, k).wait_send()

        @pl.when(z + k < 4)
        def _():
            kv_copy(k).wait_send()

    for group in range(3):
        for plane in range(4):

            @pl.when(z != plane)
            def _():
                for path in range(4):
                    xy_copy(path, group, plane).wait_send()


def front(win, wout, tok, cot, affine, bias, cosine, sine):
    rows, width = tok.shape
    chip_rows = 2 * rows
    dma = pltpu.SemaphoreType.DMA
    return pl.pallas_call(
        front_kernel,
        out_shape=(
            jax.ShapeDtypeStruct((4 * win.shape[0], win.shape[1]), BF16),
            jax.ShapeDtypeStruct((4 * wout.shape[0], wout.shape[1]), BF16),
            jax.ShapeDtypeStruct((2, rows, width), BF16),
            jax.ShapeDtypeStruct((2, rows, width), BF16),
            jax.ShapeDtypeStruct((chip_rows, width), BF16),
            jax.ShapeDtypeStruct((chip_rows, width), BF16),
            jax.ShapeDtypeStruct((HALF_D, chip_rows), BF16),
            jax.ShapeDtypeStruct((HALF_D, chip_rows), BF16),
            jax.ShapeDtypeStruct((4, chip_rows, 2 * HEAD_DIM), F32),
        ),
        in_specs=vmem_specs(8),
        out_specs=vmem_specs(9),
        scratch_shapes=[
            pltpu.VMEM((HEAD_DIM, HALF_HEADS * CHUNK), BF16),
            pltpu.VMEM((HEAD_DIM, HALF_HEADS * CHUNK), BF16),
            pltpu.VMEM((4, 2 * HEAD_DIM, CHUNK), BF16),
            pltpu.VMEM((4 * CHUNK, HEAD_DIM), BF16),
            pltpu.VMEM((4 * CHUNK, HEAD_DIM), BF16),
            pltpu.VMEM((4 * CHUNK, 2 * CHUNK), BF16),
            pltpu.VMEM((4, 1, 2 * CHUNK), F32),
            pltpu.VMEM((4 * CHUNK, HEAD_DIM), F32),
            pltpu.VMEM((4 * CHUNK, HEAD_DIM), F32),
            dma((3, 4)),
            dma((3, 4)),
            dma((4, 3, 4)),
            dma((4, 3, 4)),
            dma((2,)),
            dma((2,)),
            dma((1, 4)),
            dma((1, 4)),
            dma((4,)),
        ],
        compiler_params=pltpu.CompilerParams(
            collective_id=0, has_side_effects=True, vmem_limit_bytes=VMEM_LIMIT
        ),
        name="front",
    )(win, wout, tok, cot, affine, bias, cosine, sine)


PLANE_ORDER = (2, 1, 3, 0)
HIDDEN_BLOCK = 512
ROOT_HALF = 0.7071067811865476
GAUSS = 0.3989422804014327


def back_kernel(
    full_in,
    full_out,
    all_tok,
    all_cot,
    norm_one,
    norm_two,
    att_ref,
    dq_ref,
    dkv_part,
    affine,
    bias_up,
    bias_out,
    cos_ref,
    sin_ref,
    output_ref,
    input_grad_ref,
    sum_in,
    sum_out,
    vec_sum,
    one_t,
    two_t,
    act,
    slope,
    dhid,
    branch_t,
    qkv_grad,
    partial_out,
    upstream,
    out_other,
    up_other,
    g_in,
    g_out,
    x_in,
    x_out,
    y_in,
    y_out,
    ax_in,
    ax_out,
    ay_in,
    ay_out,
    bx_in,
    bx_out,
    by_in,
    by_out,
    t_in,
    t_out,
    z_in,
    z_out,
    own_in,
    own_out,
    vec_send,
    vec_recv,
    vec_zone,
    pair_in,
    summed,
    zone,
    dkv,
    send_sem,
    recv_sem,
    vec_send_sem,
    vec_recv_sem,
    last_send_sem,
    last_recv_sem,
    pair_send_sem,
    pair_recv_sem,
    part_send_sem,
    part_recv_sem,
    zone_send_sem,
    zone_recv_sem,
):
    z, q, c, qx, qy, xn, yn = places()
    dg = (1 - qy) * 2 + 1 - qx
    to_x, to_y, to_pair = (xn, z, c), (yn, z, c), (q, z, 1 - c)
    greet([(q, lax.rem(z + k, 4), c) for k in (1, 2, 3)] + [to_x, to_y, to_pair])
    sent = []

    def send(source, target, sems, index, device):
        copy = remote(source, target, sems[0].at[index], sems[1].at[index], device)
        copy.start()
        sent.append(copy)

    def landed(target, sems, index):
        remote(target, target, sems[0].at[index], sems[1].at[index], to_pair).wait_recv()

    main = (send_sem, recv_sem)
    vecs = (vec_send_sem, vec_recv_sem)
    lasts = (last_send_sem, last_recv_sem)
    pairs = (pair_send_sem, pair_recv_sem)
    parts = (part_send_sem, part_recv_sem)
    grads = (g_in, g_out)
    halves = tuple(ref.shape[-1] // 2 for ref in grads)
    first = tuple(pl.ds(0, half) for half in halves)
    second = tuple(pl.ds(half, half) for half in halves)
    from_x, from_y = (x_in, x_out), (y_in, y_out)
    ax, ay, bx, by = (ax_in, ax_out), (ay_in, ay_out), (bx_in, bx_out), (by_in, by_out)
    totals, zones, own = (t_in, t_out), (z_in, z_out), (own_in, own_out)
    outs = (sum_in, sum_out)
    rows = all_tok.shape[1]
    mine = pl.ds(pl.multiple_of(c * rows, rows), rows)
    other = pl.ds(pl.multiple_of((1 - c) * rows, rows), rows)
    attn_cols = HALF_D + 2 * HEAD_DIM
    hidden = full_in.shape[1] - attn_cols

    def plane_of(step):
        return lax.rem(z + PLANE_ORDER[step % 4], 4)

    def kind(step):
        return 1 if step < 4 else 0

    def exchange(step):
        h, a, j = plane_of(step), kind(step), step % 4
        if a == 1:
            size = 4 * OUT_ROWS
            left = branch_t[pl.ds(pl.multiple_of(h * size, 16), size), :]
            for half in range(2):
                cols = pl.ds(half * halves[1], halves[1])
                block = sum(
                    jnp.dot(
                        left[:, k * rows : (k + 1) * rows],
                        all_cot[k, :, cols],
                        preferred_element_type=F32,
                    )
                    for k in range(2)
                ).astype(BF16)
                for quarter in range(4):
                    g_out[h, quarter // 2, quarter % 2, :, cols] = block[
                        quarter * OUT_ROWS : (quarter + 1) * OUT_ROWS
                    ]
        else:
            size = 4 * IN_ROWS
            here = pl.ds(pl.multiple_of(h * size, 16), size)
            for number in range(4):
                cols = pl.ds(number * HIDDEN_BLOCK, HIDDEN_BLOCK)
                if number == 0:
                    block = jnp.dot(one_t[here, :], qkv_grad[...], preferred_element_type=F32)
                else:
                    block = jnp.dot(
                        two_t[here, :],
                        dhid[:, pl.ds((number - 1) * HIDDEN_BLOCK, HIDDEN_BLOCK)],
                        preferred_element_type=F32,
                    )
                block = block.astype(BF16)
                for quarter in range(4):
                    g_in[h, quarter // 2, quarter % 2, :, cols] = block[
                        quarter * IN_ROWS : (quarter + 1) * IN_ROWS
                    ]
        send(grads[a].at[h, :, 1 - qx, :, first[a]], from_x[a].at[j], main, (j, 0, a), to_x)
        send(grads[a].at[h, 1 - qy, :, :, second[a]], from_y[a].at[j], main, (j, 1, a), to_y)

    def halve(step):
        h, a, j = plane_of(step), kind(step), step % 4
        landed(from_x[a].at[j], main, (j, 0, a))
        ax[a][j] = (
            grads[a][h, 1 - qy, qx, :, first[a]].astype(F32) + from_x[a][j, 1 - qy].astype(F32)
        ).astype(BF16)
        send(ax[a].at[j], ay[a].at[j], main, (j, 2, a), to_y)
        landed(from_y[a].at[j], main, (j, 1, a))
        bx[a][j] = (
            grads[a][h, qy, 1 - qx, :, second[a]].astype(F32) + from_y[a][j, 1 - qx].astype(F32)
        ).astype(BF16)
        send(bx[a].at[j], by[a].at[j], main, (j, 3, a), to_x)

    def finish(step):
        h, a, j = plane_of(step), kind(step), step % 4
        shift = PLANE_ORDER[j]
        landed(ay[a].at[j], main, (j, 2, a))
        left = (
            grads[a][h, qy, qx, :, first[a]].astype(F32)
            + from_x[a][j, qy].astype(F32)
            + ay[a][j].astype(F32)
        )
        landed(by[a].at[j], main, (j, 3, a))
        right = (
            grads[a][h, qy, qx, :, second[a]].astype(F32)
            + from_y[a][j, qx].astype(F32)
            + by[a][j].astype(F32)
        )
        if shift == 0:
            own[a][:, first[a]] = left
            own[a][:, second[a]] = right
        else:
            totals[a][shift - 1, :, first[a]] = left.astype(BF16)
            totals[a][shift - 1, :, second[a]] = right.astype(BF16)
            send(totals[a].at[shift - 1], zones[a].at[shift - 1], main, (j, 4, a), (q, h, c))

    def share(a):
        for j in range(3):
            landed(zones[a].at[PLANE_ORDER[j] - 1], main, (j, 4, a))
        whole = own[a][...] + zones[a][0].astype(F32) + zones[a][1].astype(F32) + zones[a][2].astype(F32)
        outs[a][c, q] = whole.astype(BF16)
        piece = outs[a].at[c, q]
        send(piece, piece, lasts, (0, a), to_x)
        send(piece, piece, lasts, (1, a), to_y)
        send(piece, piece, pairs, (0, a), to_pair)

    def pass_on(a):
        piece = outs[a].at[c, xn]
        landed(piece, lasts, (0, a))
        part = outs[a].at[c, xn, :, first[a]]
        send(part, part, lasts, (2, a), to_y)
        send(piece, piece, pairs, (1, a), to_pair)
        piece = outs[a].at[c, yn]
        landed(piece, lasts, (1, a))
        part = outs[a].at[c, yn, :, second[a]]
        send(part, part, lasts, (3, a), to_x)
        send(piece, piece, pairs, (2, a), to_pair)

    def close(a):
        landed(outs[a].at[c, dg, :, first[a]], lasts, (2, a))
        landed(outs[a].at[c, dg, :, second[a]], lasts, (3, a))
        piece = outs[a].at[c, dg]
        send(piece, piece, pairs, (3, a), to_pair)

    def zone_copy(k):
        target = lax.rem(z + 4 - k, 4)
        return remote(
            summed.at[target],
            zone.at[k - 1],
            zone_send_sem.at[k],
            zone_recv_sem.at[k],
            (q, target, c),
        )

    send(dkv_part.at[:, other, :], pair_in, parts, 0, to_pair)

    branch_t[pl.ds(0, HALF_D), :] = att_ref[...]
    for number in range(hidden // HIDDEN_BLOCK):
        cols = pl.ds(number * HIDDEN_BLOCK, HIDDEN_BLOCK)
        before = (
            jnp.dot(
                norm_two[...],
                full_in[:, pl.ds(attn_cols + number * HIDDEN_BLOCK, HIDDEN_BLOCK)],
                preferred_element_type=F32,
            )
            + bias_up[:, cols]
        )
        normal = 0.5 * (1.0 + lax.erf(before * ROOT_HALF))
        active = before * normal
        act[:, cols] = active.astype(BF16)
        slope[:, cols] = normal + before * (GAUSS * jnp.exp(-0.5 * before * before))
        branch_t[pl.ds(HALF_D + number * HIDDEN_BLOCK, HIDDEN_BLOCK), :] = active.T.astype(BF16)
    exchange(0)
    exchange(1)
    landed(pair_in, parts, 0)
    for index in range(4):
        summed[index] = dkv_part[index, mine, :] + pair_in[index]
    for k in (1, 2, 3):

        @pl.when(z - k >= 0)
        def _():
            zone_copy(k).start()

    one_t[...] = norm_one[...].astype(F32).T.astype(BF16)
    two_t[...] = norm_two[...].astype(F32).T.astype(BF16)
    for number in range(hidden // HIDDEN_BLOCK):
        cols = pl.ds(number * HIDDEN_BLOCK, HIDDEN_BLOCK)
        for k in range(2):
            here = pl.ds(k * rows, rows)
            back = lax.dot_general(
                all_cot[k],
                full_out[pl.ds(HALF_D + number * HIDDEN_BLOCK, HIDDEN_BLOCK), :],
                contract_cols,
                preferred_element_type=F32,
            )
            dhid[here, cols] = (back * slope[here, cols]).astype(BF16)
    halve(0)
    exchange(2)
    dkv[mine, :] = summed[z]
    for k in (1, 2, 3):

        @pl.when(z + k < 4)
        def _():
            remote(
                zone.at[k - 1], zone.at[k - 1], zone_send_sem.at[k], zone_recv_sem.at[k], to_pair
            ).wait_recv()
            dkv[mine, :] += zone[k - 1]

    send(dkv.at[mine, :], dkv.at[mine, :], parts, 1, to_pair)
    halve(1)
    exchange(3)
    finish(0)
    partial_out[...] = jnp.dot(
        att_ref[...].astype(F32).T.astype(BF16), full_out[:HALF_D, :], preferred_element_type=F32
    ) + jnp.dot(act[...], full_out[pl.ds(HALF_D, hidden), :], preferred_element_type=F32)
    send(partial_out.at[other, :], out_other, parts, 2, to_pair)
    landed(dkv.at[other, :], parts, 1)
    half_rot = ROT // 2
    turned = dkv[...].T
    front_part, back_part = turned[:half_rot], turned[half_rot:ROT]
    cosine, sine = cos_ref[...], sin_ref[...]
    turned = jnp.concatenate(
        [
            front_part * cosine + back_part * sine,
            back_part * cosine - front_part * sine,
            turned[ROT:],
        ],
        axis=0,
    )
    qkv_grad[:, :HALF_D] = dq_ref[...].astype(F32).T.astype(BF16)
    qkv_grad[:, HALF_D:] = turned.T.astype(BF16)
    halve(2)
    exchange(4)
    finish(1)
    keep = jnp.where(c == 0, 1.0, 0.0)
    vec_send[...] = jnp.zeros_like(vec_send)
    mine_vec = vec_send.at[0]
    column = lax.broadcasted_iota(jnp.int32, (1, attn_cols), 1)
    once = jnp.where(column < HALF_D, 1.0, keep)
    first_rows = jnp.zeros((1, D), F32)
    sums = [first_rows] * 4
    for k in range(2):
        here = pl.ds(k * rows, rows)
        inputs = all_tok[k].astype(F32)
        center = inputs - jnp.mean(inputs, axis=-1, keepdims=True)
        inverse = lax.rsqrt(jnp.mean(center * center, axis=-1, keepdims=True) + 1e-05)
        normed = center * inverse
        masked = (qkv_grad[here, :].astype(F32) * once).astype(BF16)
        one = lax.dot_general(
            masked, full_in[:, :attn_cols], contract_cols, preferred_element_type=F32
        )
        two = lax.dot_general(
            dhid[here, :],
            full_in[:, pl.ds(attn_cols, hidden)],
            contract_cols,
            preferred_element_type=F32,
        )
        terms = (one * normed, one, two * normed, two)
        sums = [old + jnp.sum(term, axis=0, keepdims=True) for old, term in zip(sums, terms)]
        upstream[here, :] = one * affine[0:1, :] + two * affine[2:3, :]
    send(upstream.at[other, :], up_other, parts, 3, to_pair)
    halve(3)
    exchange(5)
    finish(2)
    for number in range(4):
        mine_vec[number : number + 1, :D] = sums[number]
    mine_vec[4:5, :D] = jnp.sum(all_cot[c].astype(F32), axis=0, keepdims=True)
    query_sums = jnp.sum(qkv_grad[...].astype(F32), axis=0, keepdims=True) * once
    hidden_sums = [
        jnp.sum(
            dhid[:, pl.ds(number * HIDDEN_BLOCK, HIDDEN_BLOCK)].astype(F32), axis=0, keepdims=True
        )
        for number in range(hidden // HIDDEN_BLOCK)
    ]
    for core in range(2):
        for number, piece in enumerate([query_sums] + hidden_sums):
            row = 4 * core + number
            mine_vec[row : row + 1, D:] = jnp.where(c == core, piece, 0.0)
    send(vec_send.at[0], vec_recv.at[0], vecs, 0, to_x)
    halve(4)
    exchange(6)
    finish(3)
    landed(vec_recv.at[0], vecs, 0)
    vec_send[1] = vec_send[0] + vec_recv[0]
    send(vec_send.at[1], vec_recv.at[1], vecs, 1, to_y)
    halve(5)
    exchange(7)
    finish(4)
    share(1)
    landed(vec_recv.at[1], vecs, 1)
    vec_send[2] = vec_send[1] + vec_recv[1]
    send(vec_send.at[2], vec_recv.at[2], vecs, 2, to_pair)
    halve(6)
    finish(5)
    pass_on(1)
    landed(vec_recv.at[2], vecs, 2)
    vec_send[3] = vec_send[2] + vec_recv[2]
    vec_zone[z] = vec_send[3]
    for k in (1, 2, 3):
        send(vec_send.at[3], vec_zone.at[z], vecs, 2 + k, (q, lax.rem(z + k, 4), c))
    halve(7)
    finish(6)
    close(1)
    landed(out_other, parts, 2)
    output_ref[...] = (
        all_tok[c].astype(F32) + (partial_out[mine, :] + out_other[...]) + bias_out[...]
    ).astype(BF16)
    landed(up_other, parts, 3)
    inputs = all_tok[c].astype(F32)
    center = inputs - jnp.mean(inputs, axis=-1, keepdims=True)
    inverse = lax.rsqrt(jnp.mean(center * center, axis=-1, keepdims=True) + 1e-05)
    normed = center * inverse
    total = upstream[mine, :] + up_other[...]
    inside = (
        total
        - jnp.mean(total, axis=-1, keepdims=True)
        - normed * jnp.mean(total * normed, axis=-1, keepdims=True)
    )
    finish(7)
    share(0)
    input_grad_ref[...] = (all_cot[c].astype(F32) + inverse * inside).astype(BF16)
    pass_on(0)
    for k in (1, 2, 3):
        landed(vec_zone.at[lax.rem(z + 4 - k, 4)], vecs, 2 + k)
    vec_sum[...] = (vec_zone[0] + vec_zone[1]) + (vec_zone[2] + vec_zone[3])
    close(0)
    for a in (1, 0):
        for index, quarter in enumerate((q, xn, yn, dg)):
            landed(outs[a].at[1 - c, quarter], pairs, (index, a))
    for copy in sent:
        copy.wait_send()
    for k in (1, 2, 3):

        @pl.when(z - k >= 0)
        def _():
            zone_copy(k).wait_send()


def back(full_in, full_out, all_tok, all_cot, norm_one, norm_two, att_t, dq_t, dkv, affine, bias_up, bias_out, cosine, sine):
    rows = all_tok.shape[1]
    chip_rows = 2 * rows
    cols_in, cols_out = full_in.shape[1], full_out.shape[1]
    hidden = bias_up.shape[1]
    kv_width = 2 * HEAD_DIM
    vec_shape = (8, D + HALF_D + kv_width)
    dma = pltpu.SemaphoreType.DMA

    def both(lead, cut, kind):
        return [
            pltpu.VMEM(lead + (IN_ROWS, cols_in // cut), kind),
            pltpu.VMEM(lead + (OUT_ROWS, cols_out // cut), kind),
        ]

    def twice(*shape):
        return [dma(shape), dma(shape)]

    return pl.pallas_call(
        back_kernel,
        out_shape=(
            jax.ShapeDtypeStruct((rows, D), BF16),
            jax.ShapeDtypeStruct((rows, D), BF16),
            jax.ShapeDtypeStruct((2, 4, IN_ROWS, cols_in), BF16),
            jax.ShapeDtypeStruct((2, 4, OUT_ROWS, cols_out), BF16),
            jax.ShapeDtypeStruct(vec_shape, F32),
        ),
        in_specs=vmem_specs(14),
        out_specs=vmem_specs(5),
        scratch_shapes=[
            pltpu.VMEM((D, chip_rows), BF16),
            pltpu.VMEM((D, chip_rows), BF16),
            pltpu.VMEM((chip_rows, hidden), BF16),
            pltpu.VMEM((chip_rows, hidden), F32),
            pltpu.VMEM((chip_rows, hidden), BF16),
            pltpu.VMEM((HALF_D + hidden, chip_rows), BF16),
            pltpu.VMEM((chip_rows, HALF_D + kv_width), BF16),
            pltpu.VMEM((chip_rows, D), F32),
            pltpu.VMEM((chip_rows, D), F32),
            pltpu.VMEM((rows, D), F32),
            pltpu.VMEM((rows, D), F32),
        ]
        + both((4, 2, 2), 1, BF16)
        + both((4, 2), 2, BF16)
        + both((4, 2), 2, BF16)
        + both((4,), 2, BF16) * 4
        + both((3,), 1, BF16) * 2
        + both((), 1, F32)
        + [
            pltpu.VMEM((4,) + vec_shape, F32),
            pltpu.VMEM((3,) + vec_shape, F32),
            pltpu.VMEM((4,) + vec_shape, F32),
            pltpu.VMEM((4, rows, kv_width), F32),
            pltpu.VMEM((4, rows, kv_width), F32),
            pltpu.VMEM((3, rows, kv_width), F32),
            pltpu.VMEM((chip_rows, kv_width), F32),
        ]
        + twice(4, 5, 2)
        + twice(6)
        + twice(4, 2)
        + twice(4, 2)
        + twice(4)
        + twice(4),
        compiler_params=pltpu.CompilerParams(
            collective_id=1, has_side_effects=True, vmem_limit_bytes=BACK_LIMIT
        ),
        name="back",
    )(full_in, full_out, all_tok, all_cot, norm_one, norm_two, att_t, dq_t, dkv, affine, bias_up, bias_out, cosine, sine)


KV_END = D + 2 * HEAD_DIM
HALF_D = D // 2


def hidden_spans(core, ff, row_share):
    spans = []
    for owner in range((D + ff) // row_share):
        first = max(owner * row_share - D, 0)
        last = (owner + 1) * row_share - D
        if last > first:
            half = (last - first) // 2
            spans.append((first + core * half, half))
    return spans


def core_columns(array, core, ff, row_share):
    pieces = [array[..., core * HALF_D : (core + 1) * HALF_D], array[..., D:KV_END]]
    pieces += [
        array[..., KV_END + first : KV_END + first + size]
        for first, size in hidden_spans(core, ff, row_share)
    ]
    return jnp.concatenate(pieces, axis=-1)


def join_columns(pair, ff, row_share):
    pieces = [pair[0][..., :HALF_D], pair[1][..., :HALF_D], pair[0][..., HALF_D : HALF_D + 2 * HEAD_DIM]]
    at = HALF_D + 2 * HEAD_DIM
    for _, size in hidden_spans(0, ff, row_share):
        pieces += [pair[0][..., at : at + size], pair[1][..., at : at + size]]
        at += size
    return jnp.concatenate(pieces, axis=-1)


def fast_shards(
    tokens,
    cotangent,
    in_master,
    in_moment,
    in_second,
    out_master,
    out_moment,
    out_second,
    vec_master,
    vec_moment,
    vec_second,
    rotary_scale,
):
    z = lax.axis_index("head")
    c = lax.axis_index("ctx")
    first_core = c == 0
    rows = tokens.shape[0]
    chip_rows = 2 * rows
    row_share = out_master.shape[0]
    ff = in_master.shape[1] - KV_END
    half_share = row_share // 2
    attn_share = D // 2

    def pick(array):
        return jnp.where(
            first_core, core_columns(array, 0, ff, row_share), core_columns(array, 1, ff, row_share)
        )

    win = pick(in_master.astype(BF16))
    out_low = out_master.astype(BF16)
    start_one = jnp.where(z == 0, attn_share * c, half_share * c)
    start_two = jnp.where(z == 0, D + (half_share - attn_share) * c, half_share * c + attn_share)
    wout = jnp.concatenate(
        [
            lax.dynamic_slice_in_dim(out_low, start_one, attn_share, 0),
            lax.dynamic_slice_in_dim(out_low, start_two, half_share - attn_share, 0),
        ],
        axis=0,
    )
    bias = pick(vec_master[5 * D :])
    attn_cols = HALF_D + 2 * HEAD_DIM
    positions = z * chip_rows + jnp.arange(chip_rows, dtype=jnp.int32)
    cosine, sine_table = rotary_tables(positions.astype(F32), rotary_scale[0].astype(F32))
    affine = vec_master[: 4 * D].reshape(4, D)
    cos_t, sin_t = cosine.T, sine_table.T
    full_in, full_out, all_tok, all_cot, norm_one, norm_two, att_t, dq_t, dkv = front(
        win,
        wout,
        tokens,
        cotangent,
        affine,
        bias[:attn_cols].reshape(1, attn_cols),
        cos_t,
        sin_t,
    )
    output, input_grad, sum_in, sum_out, sum_vec = back(
        full_in,
        full_out,
        all_tok,
        all_cot,
        norm_one,
        norm_two,
        att_t,
        dq_t,
        dkv,
        affine,
        bias[attn_cols:].reshape(1, -1),
        vec_master[4 * D : 5 * D].reshape(1, D),
        cos_t,
        sin_t,
    )
    core_sums = sum_vec[:, D:].reshape(2, -1)
    summed_vec = jnp.concatenate(
        [sum_vec[:5, :D].reshape(-1), join_columns((core_sums[0], core_sums[1]), ff, row_share)]
    )
    sum_in = sum_in.reshape(2, -1, sum_in.shape[-1])
    summed_in = join_columns((sum_in[0], sum_in[1]), ff, row_share).astype(F32)
    low, high = sum_out.reshape(2, half_share, D)
    head_rows = jnp.concatenate([low[:attn_share], high[:attn_share], low[attn_share:], high[attn_share:]], axis=0)
    summed_out = jnp.where(z == 0, head_rows, jnp.concatenate([low, high], axis=0)).astype(F32)

    in_moment_new, in_second_new, in_master_new = adam_update(
        in_master, in_moment, in_second, summed_in, matrix_rate, weight_decay
    )
    out_moment_new, out_second_new, out_master_new = adam_update(
        out_master, out_moment, out_second, summed_out, matrix_rate, weight_decay
    )
    vec_moment_new, vec_second_new, vec_master_new = adam_update(
        vec_master, vec_moment, vec_second, summed_vec, vector_rate, 0.0
    )
    return (
        output,
        input_grad,
        in_moment_new,
        in_second_new,
        in_master_new,
        in_master_new.astype(BF16),
        out_moment_new,
        out_second_new,
        out_master_new,
        out_master_new.astype(BF16),
        vec_moment_new,
        vec_second_new,
        vec_master_new,
    )


def solution(mesh):
    placed = (
        P(("dp", "head", "ctx"), None),
        P(("dp", "head", "ctx"), None),
        P("head", None),
        P("head", None),
        P("head", None),
        P("head", None),
        P("head", None),
        P("head", None),
        P(),
        P(),
        P(),
        P(),
    )
    paired = dict(mesh.shape) == {"dp": 4, "head": 4, "ctx": 2}
    body = fast_shards if paired else shards
    return jax.shard_map(
        body,
        mesh=mesh,
        in_specs=placed,
        out_specs=(
            P(("dp", "head", "ctx"), None),
            P(("dp", "head", "ctx"), None),
            P("head", None),
            P("head", None),
            P("head", None),
            P("head", None),
            P("head", None),
            P("head", None),
            P("head", None),
            P("head", None),
            P(),
            P(),
            P(),
        ),
        check_vma=False,
    )
```

profile of v0, /device:TPU:0, one launch (start us, length us, event | category | flops | bytes accessed | tf_op | source)
XLA Modules:
  0.0 229.7 jit_solution(11185438856043530481)
XLA Ops:
  1.3 0.8 slice.209
  2.1 0.7 slice.204
  2.8 0.7 slice.208
  3.5 0.7 slice.203
  4.2 0.7 slice.215
  5.4 0.7 slice.202
  6.8 0.9 fusion.13
  9.0 0.8 multiply_sine_fusion
  9.8 2.1 convert_element_type.32
  12.0 0.9 pad_maximum_fusion.wout
  13.7 0.6 concatenate.34
  14.9 1.0 broadcast_select_fusion.win
  15.9 70.9 %front.1 = (bf16[768,2048]{1,0:T(8,128)(2,1)}, bf16[1920,768]{1,0:T(8,128)(2,1)}, bf16[2,256,768]{2,1,0:T(8,128)(2,1)}, bf16[2,256,768]{2,1,0:T(8,128)(2,1)}, bf...) custom-call(bf16[192,2048]{1,0:T(8,128)(2,1)} %broadcast_select_fusi, ...), custom_call_target="tpu_custom_call" | custom-call | tf_op jit(solution)/shard_map/front/pallas_call | solution.py:713
  86.8 110.9 %back.1 = (bf16[256,768]{1,0:T(8,128)(2,1)}, bf16[256,768]{1,0:T(8,128)(2,1)}, bf16[2,4,48,2048]{3,2,1,0:T(8,128)(2,1)}, bf16[2,4,120,768]{3,2,1,0:T(8,128)(2,1)}, f32[8,1280]{1,0:T(8,128)}) custom-call(bf16[768,2048]{1,0:T(8,128)(2,1)} %get-tuple-element.27.full_in, bf16[1920,768]{1,0:T(8,128)(2,1)} %get-tuple-element.28.full_out, ...), custom_call_target="tpu_custom_call" | custom-call | tf_op jit(solution)/shard_map/back/pallas_call | solution.py:1187
  197.8 0.8 slice_bitcast_fusion
  198.6 0.7 slice.232
  199.6 1.4 multiply_subtract_fusion.2
  201.0 1.6 fusion.10
  202.6 0.7 slice.270
  203.3 0.7 slice.269
  204.0 0.9 slice.267
  205.7 0.6 slice.259
  206.4 0.7 slice.257
  207.0 0.7 slice.258
  207.7 1.6 fusion.11
  209.3 4.1 %concatenate.38 = bf16[192,3968]{1,0:T(8,128)(2,1)} concatenate(bf16[192,384]{1,0:T(8,128)(2,1)} %slice.257, bf16[192,384]{1,0:T(8,128)(2,1)} %slice.258, bf16[192,224]{1,0:T(8,128)(2,1)} %slice.259, bf16[192,96]{1,0:T(8,128)(2,1)} %slice.260, bf16[192,480]{1,0:T(8,128)(2,1)} %get-tuple-element.84, bf16[192,480]{1,0:T(8,128)(2,1)} %get-tuple-element.64, ...), dimensions={1} | concatenate | bytes 3047424 | tf_op jit(solution)/shard_map/concatenate | solution.py:1269
  213.5 8.0 %fusion.4 = (bf16[960,768]{1,0:T(8,128)(2,1)}, f32[960,768]{1,0:T(8,128)}, f32[960,768]{1,0:T(8,128)}, f32[960,768]{1,0:T(8,128)}) fusion(f32[960,768]{1,0:T(8,128)S(1)} %copy-done.2, bf16[480,768]{1,0:T(8,128)(2,1)} %bitcast.17, bf16[480,768]{1,0:T(8,128)(2,1)} %bitcast.14, bf16[96,768]{1,0:T(8,128)(2,1)} %slice.270, bf16[96,768]{1,0:T(8,128)(2,1)} %slice.269, ...), kind=kLoop, calls=%fused_computation.24 | loop fusion | flops 21381120 | bytes 22118400 | tf_op jit(solution)/shard_map/convert_element_type | solution.py:1373
  221.5 1.1 copy-done.6
  222.6 0.9 copy-done.7
  223.5 4.7 %fusion.6 = (bf16[192,3968]{1,0:T(8,128)(2,1)}, f32[192,3968]{1,0:T(8,128)}, f32[192,3968]{1,0:T(8,128)}, f32[192,3968]{1,0:T(8,128)}) fusion(f32[192,3968]{1,0:T(8,128)S(1)} %copy-done.1, bf16[192,3968]{1,0:T(8,128)(2,1)S(1)} %copy-done.5, f32[192,3968]{1,0:T(8,128)S(1)} %copy-done.6, f32[192,3968]{1,0:T(8,128)S(1)} %copy-done.7), kind=kLoop, calls=%fused_computation.25 | loop fusion | flops 12189696 | bytes 21331968 | tf_op jit(solution)/shard_map/convert_element_type | solution.py:1369
  228.2 0.7 copy.30
  229.0 0.7 copy.31
  (53 shorter events, 5.1 us)
Async XLA Ops:
  9.8 3.1 %copy-start = (f32[192,3968]{1,0:T(8,128)S(1)}, f32[192,3968]{1,0:T(8,128)}, u32[]{:S(2)}) copy-start(f32[192,3968]{1,0:T(8,128)} %param.14) | copy-start | bytes 9142276
  86.8 112.7 %copy-start.11 = (f32[7808]{0:T(1024)S(1)}, f32[7808]{0:T(1024)}, u32[]{:S(2)}) copy-start(f32[7808]{0:T(1024)} %param.20) | copy-start | bytes 93700
  201.0 3.9 %copy-start.8 = (bf16[2,4,48,2048]{3,2,1,0:T(8,128)(2,1)S(1)}, bf16[2,4,48,2048]{3,2,1,0:T(8,128)(2,1)}, u32[]{:S(2)}) copy-start(bf16[2,4,48,2048]{3,2,1,0:T(8,128)(2,1)} %get-tuple-element.38) | copy-start | bytes 4718596
  202.6 2.5 %copy-start.3 = (bf16[1,4,120,768]{3,2,1,0:T(8,128)(2,1)}, bf16[1,4,120,768]{3,2,1,0:T(8,128)(2,1)S(1)}, u32[]{:S(2)}) copy-start(bf16[1,4,120,768]{3,2,1,0:T(8,128)(2,1)S(1)} %get-tuple-element.60) | copy-start | bytes 2211844
  202.6 2.5 %copy-start.4 = (bf16[1,4,120,768]{3,2,1,0:T(8,128)(2,1)}, bf16[1,4,120,768]{3,2,1,0:T(8,128)(2,1)S(1)}, u32[]{:S(2)}) copy-start(bf16[1,4,120,768]{3,2,1,0:T(8,128)(2,1)S(1)} %get-tuple-element.61) | copy-start | bytes 2211844
  207.0 6.4 %copy-start.2 = (f32[960,768]{1,0:T(8,128)S(1)}, f32[960,768]{1,0:T(8,128)}, u32[]{:S(2)}) copy-start(f32[960,768]{1,0:T(8,128)} %param.17) | copy-start | bytes 8847364
  213.4 8.1 %copy-start.1 = (f32[192,3968]{1,0:T(8,128)S(1)}, f32[192,3968]{1,0:T(8,128)}, u32[]{:S(2)}) copy-start(f32[192,3968]{1,0:T(8,128)} %param.14) | copy-start | bytes 9142276
  213.4 8.1 %copy-start.5 = (bf16[192,3968]{1,0:T(8,128)(2,1)S(1)}, bf16[192,3968]{1,0:T(8,128)(2,1)}, u32[]{:S(2)}) copy-start(bf16[192,3968]{1,0:T(8,128)(2,1)} %concatenate.38) | copy-start | bytes 4571140
  213.4 9.2 %copy-start.6 = (f32[192,3968]{1,0:T(8,128)S(1)}, f32[192,3968]{1,0:T(8,128)}, u32[]{:S(2)}) copy-start(f32[192,3968]{1,0:T(8,128)} %param.16) | copy-start | bytes 9142276
  213.4 10.1 %copy-start.7 = (f32[192,3968]{1,0:T(8,128)S(1)}, f32[192,3968]{1,0:T(8,128)}, u32[]{:S(2)}) copy-start(f32[192,3968]{1,0:T(8,128)} %param.15) | copy-start | bytes 9142276
  223.5 4.7 %copy-start.10 = (bf16[256,768]{1,0:T(8,128)(2,1)S(1)}, bf16[256,768]{1,0:T(8,128)(2,1)}, u32[]{:S(2)}) copy-start(bf16[256,768]{1,0:T(8,128)(2,1)} %get-tuple-element.103) | copy-start | bytes 1179652
  223.5 5.5 %copy-start.9 = (bf16[256,768]{1,0:T(8,128)(2,1)S(1)}, bf16[256,768]{1,0:T(8,128)(2,1)}, u32[]{:S(2)}) copy-start(bf16[256,768]{1,0:T(8,128)(2,1)} %get-tuple-element.104) | copy-start | bytes 1179652
where the time goes:
time: 231 us; the launch traced here: 230 us
  Pallas kernels  182 us (79%)
  local copies, waits for them, and re-layouts  27.2 us (12%)
  other arithmetic  19.1 us (8%)
    pallas_call x1, Pallas kernels, back(): pl.pallas_call(back_kernel, out_shape=(jax.ShapeDtypeStruct((rows, D), BF...  111 us
    pallas_call x1, Pallas kernels, front(): pl.pallas_call(front_kernel, out_shape=(jax.ShapeDtypeStruct((4 * win.sha...  70.9 us
    convert_element_type x1, other arithmetic, fast_shards(): out_master_new.astype(BF16)  8.04 us
    convert_element_type x1, other arithmetic, fast_shards(): in_master_new.astype(BF16)  4.72 us

commit v1 on v0

--- a/solution.py
+++ b/solution.py
@@ -367,18 +367,59 @@
     )
 
 
+KV_END = D + 2 * HEAD_DIM
+HALF_D = D // 2
+
+
+def hidden_spans(core, ff, row_share):
+    spans = []
+    for owner in range((D + ff) // row_share):
+        first = max(owner * row_share - D, 0)
+        last = (owner + 1) * row_share - D
+        if last > first:
+            half = (last - first) // 2
+            spans.append((first + core * half, half))
+    return spans
+
+
+def core_columns(array, core, ff, row_share):
+    pieces = [array[..., core * HALF_D : (core + 1) * HALF_D], array[..., D:KV_END]]
+    pieces += [
+        array[..., KV_END + first : KV_END + first + size]
+        for first, size in hidden_spans(core, ff, row_share)
+    ]
+    return jnp.concatenate(pieces, axis=-1)
+
+
+def join_columns(pair, ff, row_share):
+    pieces = [pair[0][..., :HALF_D], pair[1][..., :HALF_D], pair[0][..., HALF_D : HALF_D + 2 * HEAD_DIM]]
+    at = HALF_D + 2 * HEAD_DIM
+    for _, size in hidden_spans(0, ff, row_share):
+        pieces += [pair[0][..., at : at + size], pair[1][..., at : at + size]]
+        at += size
+    return jnp.concatenate(pieces, axis=-1)
+
+
 CHUNK = 512
 IN_ROWS = 48
 OUT_ROWS = 120
 
 
+def core_bias(vec, c, first, last):
+    ff = vec.shape[1] - 5 * D - KV_END
+    share = (D + ff) // 4
+    tail = vec[:, 5 * D :]
+    return jnp.where(
+        c == 0, core_columns(tail, 0, ff, share), core_columns(tail, 1, ff, share)
+    )[:, first:last]
+
+
 def front_kernel(
-    win,
-    wout,
+    in_master,
+    out_master,
     tok,
     cot,
-    affine,
-    bias,
+    vec,
     cos_ref,
     sin_ref,
     full_in,
@@ -414,8 +455,7 @@
     to_x, to_y, to_pair = (xn, z, c), (yn, z, c), (q, z, 1 - c)
     greet([(q, lax.rem(z + k, 4), c) for k in (1, 2, 3)] + [to_x, to_y, to_pair])
     attn_cols = HALF_D + 2 * HEAD_DIM
-    groups = ((0, 0, attn_cols), (1, 0, D), (0, attn_cols, win.shape[1]))
-    own = (win, wout)
+    groups = ((0, 0, attn_cols), (1, 0, D), (0, attn_cols, full_in.shape[1]))
     full = (full_in, full_out)
     piece_rows = (IN_ROWS, OUT_ROWS)
 
@@ -436,15 +476,21 @@
         which, cols = span(group, part)
         return full[which].at[rows_of(which, plane, quarter), cols]
 
-    def z_copy(group, k):
-        which, cols = span(group, 0)
+    def z_copy(group, plane, way):
+        piece = place(group, 0, plane, q)
         return remote(
-            own[which].at[rows_of(which, 0, q), cols],
-            place(group, 0, z, q),
-            z_send.at[group, k],
-            z_recv.at[group, z],
-            (q, lax.rem(z + k, 4), c),
-        )
+            piece, piece, z_send.at[group, plane, way], z_recv.at[group, plane], (q, z + 1 - 2 * way, c)
+        )
+
+    def z_room(way):
+        return z < 3 if way == 0 else z > 0
+
+    def z_start(group):
+        for way in range(2):
+
+            @pl.when(z_room(way))
+            def _():
+                z_copy(group, z, way).start()
 
     def pair_copy(number):
         source, target = ((tok, all_tok), (cot, all_cot))[number]
@@ -452,19 +498,8 @@
 
     for number in range(2):
         pair_copy(number).start()
-    for group in range(3):
-        for k in (1, 2, 3):
-            z_copy(group, k).start()
-
     locals_ = []
-    for number, (source, target) in enumerate(
-        (
-            (win, full_in.at[pl.ds(pl.multiple_of(z * 4 * IN_ROWS, 8), 4 * IN_ROWS), :]),
-            (wout, full_out.at[pl.ds(pl.multiple_of(z * 4 * OUT_ROWS, 8), 4 * OUT_ROWS), :]),
-            (tok, all_tok.at[c]),
-            (cot, all_cot.at[c]),
-        )
-    ):
+    for number, (source, target) in enumerate(((tok, all_tok.at[c]), (cot, all_cot.at[c]))):
         copy = pltpu.make_async_copy(source, target, local_sem.at[number])
         copy.start()
         locals_.append(copy)
@@ -487,49 +522,96 @@
             piece, piece, xy_send.at[path, group, plane], xy_recv.at[path, group, plane], to_pair
         ).wait_recv()
 
-    def spread(group, plane):
-        @pl.when(z != plane)
-        def _():
-            piece = place(group, 0, plane, q)
-            remote(piece, piece, z_send.at[group, 1], z_recv.at[group, plane], to_pair).wait_recv()
-            xy_copy(0, group, plane).start()
-            xy_copy(1, group, plane).start()
-
-    def relay(group, plane):
-        @pl.when(z != plane)
-        def _():
+    row_share = out_master.shape[0]
+    ff = in_master.shape[1] - KV_END
+    for quarter in range(4):
+        block = in_master[quarter * IN_ROWS : (quarter + 1) * IN_ROWS, :]
+        full_in[rows_of(0, z, quarter), :] = jnp.where(
+            c == 0, core_columns(block, 0, ff, row_share), core_columns(block, 1, ff, row_share)
+        ).astype(BF16)
+    z_start(0)
+    half_share = row_share // 2
+    begin = jnp.where(z == 0, HALF_D * c, half_share * c)
+    begin_tail = jnp.where(z == 0, D + (half_share - HALF_D) * c, half_share * c + HALF_D)
+    base_row = pl.multiple_of(z * half_share, 16)
+    full_out[pl.ds(base_row, HALF_D), :] = out_master[
+        pl.ds(pl.multiple_of(begin, 8), HALF_D), :
+    ].astype(BF16)
+    full_out[pl.ds(pl.multiple_of(base_row + HALF_D, 16), half_share - HALF_D), :] = out_master[
+        pl.ds(pl.multiple_of(begin_tail, 8), half_share - HALF_D), :
+    ].astype(BF16)
+    z_start(1)
+    z_start(2)
+
+    def spread(group, far):
+        for way in range(2):
+            plane = z - far if way == 0 else z + far
+
+            @pl.when(plane >= 0 if way == 0 else plane < 4)
+            def _():
+                piece = place(group, 0, plane, q)
+                remote(
+                    piece, piece, z_send.at[group, plane, way], z_recv.at[group, plane], to_pair
+                ).wait_recv()
+
+                @pl.when(z_room(way))
+                def _():
+                    z_copy(group, plane, way).start()
+
+                xy_copy(0, group, plane).start()
+                xy_copy(1, group, plane).start()
+
+    def either(far, work):
+        for way in range(2):
+            plane = z - far if way == 0 else z + far
+
+            @pl.when(plane >= 0 if way == 0 else plane < 4)
+            def _():
+                work(plane)
+
+    def relay(group, far):
+        def work(plane):
             xy_landed(0, group, plane)
             xy_copy(2, group, plane).start()
             xy_landed(1, group, plane)
             xy_copy(3, group, plane).start()
 
-    def settle(group, plane):
-        @pl.when(z != plane)
-        def _():
+        either(far, work)
+
+    def settle(group):
+        def work(plane):
             xy_landed(2, group, plane)
             xy_landed(3, group, plane)
 
-    locals_[2].wait()
-    locals_[3].wait()
-    for number, target in enumerate((all_tok, all_cot)):
-        piece = target.at[1 - c]
-        remote(piece, piece, pair_send.at[number], pair_recv.at[number], to_pair).wait_recv()
+        for far in (1, 2, 3):
+            either(far, work)
+
     rows = tok.shape[0]
-    for half in range(2):
+
+    def normalize(half):
         inputs = all_tok[half].astype(F32)
         center = inputs - jnp.mean(inputs, axis=-1, keepdims=True)
         inverse = lax.rsqrt(jnp.mean(center * center, axis=-1, keepdims=True) + 1e-05)
         normed = center * inverse
-        norm_one[pl.ds(half * rows, rows), :] = (normed * affine[0:1, :] + affine[1:2, :]).astype(BF16)
-        norm_two[pl.ds(half * rows, rows), :] = (normed * affine[2:3, :] + affine[3:4, :]).astype(BF16)
-    for plane in range(4):
-        spread(0, plane)
-    for plane in range(4):
-        relay(0, plane)
-    for plane in range(4):
-        settle(0, plane)
-    locals_[0].wait()
-    locals_[1].wait()
+        here = pl.ds(pl.multiple_of(half * rows, rows), rows)
+        norm_one[here, :] = (normed * vec[:, :D] + vec[:, D : 2 * D]).astype(BF16)
+        norm_two[here, :] = (normed * vec[:, 2 * D : 3 * D] + vec[:, 3 * D : 4 * D]).astype(BF16)
+
+    for copy in locals_:
+        copy.wait()
+    normalize(c)
+    spread(0, 1)
+    for number, target in enumerate((all_tok, all_cot)):
+        piece = target.at[1 - c]
+        remote(piece, piece, pair_send.at[number], pair_recv.at[number], to_pair).wait_recv()
+    normalize(1 - c)
+    spread(0, 2)
+    relay(0, 1)
+    spread(0, 3)
+    relay(0, 2)
+    spread(1, 1)
+    relay(0, 3)
+    settle(0)
 
     half_rot = ROT // 2
     cosine, sine = cos_ref[...], sin_ref[...]
@@ -541,7 +623,8 @@
         )
 
     projected = (
-        jnp.dot(norm_one[...], full_in[:, :attn_cols], preferred_element_type=F32) + bias[...]
+        jnp.dot(norm_one[...], full_in[:, :attn_cols], preferred_element_type=F32)
+        + core_bias(vec, c, 0, attn_cols)
     ).T
     key_t = turn(projected[HALF_D : HALF_D + HEAD_DIM], cosine, sine)
     kv_all[z] = jnp.concatenate([key_t, projected[HALF_D + HEAD_DIM :]], axis=0).astype(BF16)
@@ -560,7 +643,7 @@
     for head in range(HALF_HEADS):
         block = turn(projected[head * HEAD_DIM : (head + 1) * HEAD_DIM], cosine, sine) * 0.125
         q_all[:, head * CHUNK : (head + 1) * CHUNK] = block.astype(BF16)
-    spread(1, 0)
+    spread(1, 2)
     dkeys[...] = jnp.zeros_like(dkeys)
     dvalues[...] = jnp.zeros_like(dvalues)
 
@@ -571,7 +654,7 @@
         values[place_rows, :] = turned[:, HEAD_DIM:]
 
     spread_block(z)
-    relay(1, 0)
+    relay(1, 1)
     for k in (1, 2, 3):
 
         @pl.when(z - k >= 0)
@@ -582,43 +665,41 @@
             ).wait_recv()
             spread_block(source)
 
-    settle(1, 0)
-    grads_t = jnp.concatenate(
-        [
-            lax.dot_general(
-                full_out[:HALF_D, :], all_cot[half], contract_cols, preferred_element_type=F32
-            )
-            for half in range(2)
-        ],
-        axis=1,
-    ).astype(BF16)
-    for head in range(HALF_HEADS):
-        g_all[:, head * CHUNK : (head + 1) * CHUNK] = grads_t[head * HEAD_DIM : (head + 1) * HEAD_DIM]
-
     width = 2 * CHUNK
     cos_two = jnp.concatenate([cosine, cosine], axis=1)
     sin_two = jnp.concatenate([sine, sine], axis=1)
-    polls = (
-        ((spread, 1, 1), (spread, 1, 2)),
-        ((relay, 1, 1), (relay, 1, 2), (spread, 1, 3)),
-        ((relay, 1, 3), (spread, 2, 0)),
-        ((relay, 2, 0), (spread, 2, 1), (spread, 2, 2)),
-        ((relay, 2, 1), (relay, 2, 2), (spread, 2, 3)),
-        ((relay, 2, 3),),
-    )
-
-    def poll(pair, late):
-        for number in range(3):
-
-            @pl.when(pair == number)
-            def _():
-                for action, group, plane in polls[2 * number + late]:
-                    action(group, plane)
+    polls = {
+        (0, 0, 0): ((spread, 1, 3),),
+        (0, 0, 1): ((relay, 1, 2),),
+        (0, 0, 3): ((spread, 2, 1),),
+        (0, 1, 0): ((spread, 2, 2),),
+        (0, 1, 2): ((relay, 2, 1), (spread, 2, 3)),
+        (1, 0, 1): ((relay, 2, 2),),
+        (1, 1, 0): ((relay, 2, 3),),
+    }
+
+    def poll(pair, late, index):
+        for (number, phase, chunk), work in polls.items():
+            if phase == late:
+
+                @pl.when(jnp.logical_and(pair == number, index == chunk))
+                def _():
+                    for action, group, far in work:
+                        action(group, far)
+
+    def upstream_heads():
+        relay(1, 3)
+        settle(1)
+        for head in range(HALF_HEADS):
+            part = full_out[pl.ds(head * HEAD_DIM, HEAD_DIM), :]
+            for half in range(2):
+                g_all[:, pl.ds(head * CHUNK + half * rows, rows)] = lax.dot_general(
+                    part, all_cot[half], contract_cols, preferred_element_type=F32
+                ).astype(BF16)
 
     def two_heads(pair, carry):
         cols = pl.ds(pl.multiple_of(pair * width, width), width)
         queries = q_all[:, cols]
-        grads = g_all[:, cols].astype(F32)
 
         def rows_at(index):
             return pl.ds(pl.multiple_of(index * CHUNK, CHUNK), CHUNK)
@@ -647,7 +728,14 @@
             jnp.zeros((1, width), F32),
             jnp.zeros((HEAD_DIM, width), F32),
         )
-        state = lax.fori_loop(0, z, lambda index, state: forward(index, state, False), state)
+
+        def forward_or_not(index, state):
+            poll(pair, 0, index)
+            return lax.cond(
+                index < z, lambda old: forward(index, old, False), lambda old: old, state
+            )
+
+        state = lax.fori_loop(0, 4, forward_or_not, state)
         top, total, out = forward(z, state, True)
         inverse = 1.0 / total
         out = out * inverse
@@ -655,8 +743,9 @@
         second = pl.multiple_of(base + HEAD_DIM, HEAD_DIM)
         att_ref[pl.ds(base, HEAD_DIM), :] = out[:, :CHUNK].astype(BF16)
         att_ref[pl.ds(second, HEAD_DIM), :] = out[:, CHUNK:].astype(BF16)
+        pl.when(pair == 0)(upstream_heads)
+        grads = g_all[:, cols].astype(F32)
         inner = jnp.sum(grads * out, axis=0, keepdims=True)
-        poll(pair, 0)
 
         def backward(index, dq):
             here = rows_at(index)
@@ -673,11 +762,14 @@
             )
             return dq + jnp.dot(kv_all[index, :HEAD_DIM, :], dscore, preferred_element_type=F32)
 
-        dq = lax.fori_loop(0, z + 1, backward, jnp.zeros((HEAD_DIM, width), F32))
+        def backward_or_not(index, dq):
+            poll(pair, 1, index)
+            return lax.cond(index <= z, lambda old: backward(index, old), lambda old: old, dq)
+
+        dq = lax.fori_loop(0, 4, backward_or_not, jnp.zeros((HEAD_DIM, width), F32))
         dq = turn(dq * 0.125, cos_two, -sin_two)
         dq_ref[pl.ds(base, HEAD_DIM), :] = dq[:, :CHUNK].astype(BF16)
         dq_ref[pl.ds(second, HEAD_DIM), :] = dq[:, CHUNK:].astype(BF16)
-        poll(pair, 1)
         return carry
 
     lax.fori_loop(0, HALF_HEADS // 2, two_heads, 0)
@@ -685,19 +777,29 @@
     for index in range(4):
         here = pl.ds(index * CHUNK, CHUNK)
         dkv_ref[index] = jnp.concatenate([dkeys[here, :], dvalues[here, :]], axis=1)
-    for group, plane in ((1, 1), (1, 2), (1, 3), (2, 0), (2, 1), (2, 2), (2, 3)):
-        settle(group, plane)
+    settle(2)
     for number in range(2):
         pair_copy(number).wait_send()
     for k in (1, 2, 3):
-        for group in range(3):
-            z_copy(group, k).wait_send()
 
         @pl.when(z + k < 4)
         def _():
             kv_copy(k).wait_send()
 
     for group in range(3):
+        for way in range(2):
+
+            @pl.when(z_room(way))
+            def _():
+                z_copy(group, z, way).wait_send()
+
+                for far in (1, 2, 3):
+                    plane = z - far if way == 0 else z + far
+
+                    @pl.when(plane >= 0 if way == 0 else plane < 4)
+                    def _():
+                        z_copy(group, plane, way).wait_send()
+
         for plane in range(4):
 
             @pl.when(z != plane)
@@ -706,15 +808,16 @@
                     xy_copy(path, group, plane).wait_send()
 
 
-def front(win, wout, tok, cot, affine, bias, cosine, sine):
+def front(in_master, out_master, tok, cot, vec, cosine, sine):
     rows, width = tok.shape
+    core_cols = (in_master.shape[1] + 2 * HEAD_DIM) // 2
     chip_rows = 2 * rows
     dma = pltpu.SemaphoreType.DMA
     return pl.pallas_call(
         front_kernel,
         out_shape=(
-            jax.ShapeDtypeStruct((4 * win.shape[0], win.shape[1]), BF16),
-            jax.ShapeDtypeStruct((4 * wout.shape[0], wout.shape[1]), BF16),
+            jax.ShapeDtypeStruct((4 * in_master.shape[0], core_cols), BF16),
+            jax.ShapeDtypeStruct((2 * out_master.shape[0], width), BF16),
             jax.ShapeDtypeStruct((2, rows, width), BF16),
             jax.ShapeDtypeStruct((2, rows, width), BF16),
             jax.ShapeDtypeStruct((chip_rows, width), BF16),
@@ -723,7 +826,7 @@
             jax.ShapeDtypeStruct((HALF_D, chip_rows), BF16),
             jax.ShapeDtypeStruct((4, chip_rows, 2 * HEAD_DIM), F32),
         ),
-        in_specs=vmem_specs(8),
+        in_specs=vmem_specs(7),
         out_specs=vmem_specs(9),
         scratch_shapes=[
             pltpu.VMEM((HEAD_DIM, HALF_HEADS * CHUNK), BF16),
@@ -735,7 +838,7 @@
             pltpu.VMEM((4, 1, 2 * CHUNK), F32),
             pltpu.VMEM((4 * CHUNK, HEAD_DIM), F32),
             pltpu.VMEM((4 * CHUNK, HEAD_DIM), F32),
-            dma((3, 4)),
+            dma((3, 4, 2)),
             dma((3, 4)),
             dma((4, 3, 4)),
             dma((4, 3, 4)),
@@ -743,13 +846,13 @@
             dma((2,)),
             dma((1, 4)),
             dma((1, 4)),
-            dma((4,)),
+            dma((2,)),
         ],
         compiler_params=pltpu.CompilerParams(
             collective_id=0, has_side_effects=True, vmem_limit_bytes=VMEM_LIMIT
         ),
         name="front",
-    )(win, wout, tok, cot, affine, bias, cosine, sine)
+    )(in_master, out_master, tok, cot, vec, cosine, sine)
 
 
 PLANE_ORDER = (2, 1, 3, 0)
@@ -768,9 +871,7 @@
     att_ref,
     dq_ref,
     dkv_part,
-    affine,
-    bias_up,
-    bias_out,
+    vec_ref,
     cos_ref,
     sin_ref,
     output_ref,
@@ -985,6 +1086,7 @@
     send(dkv_part.at[:, other, :], pair_in, parts, 0, to_pair)
 
     branch_t[pl.ds(0, HALF_D), :] = att_ref[...]
+    bias_up = core_bias(vec_ref, c, attn_cols, attn_cols + hidden)
     for number in range(hidden // HIDDEN_BLOCK):
         cols = pl.ds(number * HIDDEN_BLOCK, HIDDEN_BLOCK)
         before = (
@@ -993,7 +1095,7 @@
                 full_in[:, pl.ds(attn_cols + number * HIDDEN_BLOCK, HIDDEN_BLOCK)],
                 preferred_element_type=F32,
             )
-            + bias_up[:, cols]
+            + bias_up[:, number * HIDDEN_BLOCK : (number + 1) * HIDDEN_BLOCK]
         )
         normal = 0.5 * (1.0 + lax.erf(before * ROOT_HALF))
         active = before * normal
@@ -1087,7 +1189,7 @@
         )
         terms = (one * normed, one, two * normed, two)
         sums = [old + jnp.sum(term, axis=0, keepdims=True) for old, term in zip(sums, terms)]
-        upstream[here, :] = one * affine[0:1, :] + two * affine[2:3, :]
+        upstream[here, :] = one * vec_ref[:, :D] + two * vec_ref[:, 2 * D : 3 * D]
     send(upstream.at[other, :], up_other, parts, 3, to_pair)
     halve(3)
     exchange(5)
@@ -1133,7 +1235,7 @@
     close(1)
     landed(out_other, parts, 2)
     output_ref[...] = (
-        all_tok[c].astype(F32) + (partial_out[mine, :] + out_other[...]) + bias_out[...]
+        all_tok[c].astype(F32) + (partial_out[mine, :] + out_other[...]) + vec_ref[:, 4 * D : 5 * D]
     ).astype(BF16)
     landed(up_other, parts, 3)
     inputs = all_tok[c].astype(F32)
@@ -1166,11 +1268,11 @@
             zone_copy(k).wait_send()
 
 
-def back(full_in, full_out, all_tok, all_cot, norm_one, norm_two, att_t, dq_t, dkv, affine, bias_up, bias_out, cosine, sine):
+def back(full_in, full_out, all_tok, all_cot, norm_one, norm_two, att_t, dq_t, dkv, vec, cosine, sine):
     rows = all_tok.shape[1]
     chip_rows = 2 * rows
     cols_in, cols_out = full_in.shape[1], full_out.shape[1]
-    hidden = bias_up.shape[1]
+    hidden = cols_in - HALF_D - 2 * HEAD_DIM
     kv_width = 2 * HEAD_DIM
     vec_shape = (8, D + HALF_D + kv_width)
     dma = pltpu.SemaphoreType.DMA
@@ -1193,7 +1295,7 @@
             jax.ShapeDtypeStruct((2, 4, OUT_ROWS, cols_out), BF16),
             jax.ShapeDtypeStruct(vec_shape, F32),
         ),
-        in_specs=vmem_specs(14),
+        in_specs=vmem_specs(12),
         out_specs=vmem_specs(5),
         scratch_shapes=[
             pltpu.VMEM((D, chip_rows), BF16),
@@ -1233,40 +1335,102 @@
             collective_id=1, has_side_effects=True, vmem_limit_bytes=BACK_LIMIT
         ),
         name="back",
-    )(full_in, full_out, all_tok, all_cot, norm_one, norm_two, att_t, dq_t, dkv, affine, bias_up, bias_out, cosine, sine)
-
-
-KV_END = D + 2 * HEAD_DIM
-HALF_D = D // 2
-
-
-def hidden_spans(core, ff, row_share):
-    spans = []
-    for owner in range((D + ff) // row_share):
-        first = max(owner * row_share - D, 0)
-        last = (owner + 1) * row_share - D
-        if last > first:
-            half = (last - first) // 2
-            spans.append((first + core * half, half))
-    return spans
-
-
-def core_columns(array, core, ff, row_share):
-    pieces = [array[..., core * HALF_D : (core + 1) * HALF_D], array[..., D:KV_END]]
-    pieces += [
-        array[..., KV_END + first : KV_END + first + size]
-        for first, size in hidden_spans(core, ff, row_share)
-    ]
-    return jnp.concatenate(pieces, axis=-1)
-
-
-def join_columns(pair, ff, row_share):
-    pieces = [pair[0][..., :HALF_D], pair[1][..., :HALF_D], pair[0][..., HALF_D : HALF_D + 2 * HEAD_DIM]]
-    at = HALF_D + 2 * HEAD_DIM
-    for _, size in hidden_spans(0, ff, row_share):
-        pieces += [pair[0][..., at : at + size], pair[1][..., at : at + size]]
-        at += size
-    return jnp.concatenate(pieces, axis=-1)
+    )(full_in, full_out, all_tok, all_cot, norm_one, norm_two, att_t, dq_t, dkv, vec, cosine, sine)
+
+
+ADAM_ROWS = 32
+ADAM_OUT_ROWS = 96
+
+
+def adam_in_kernel(
+    grad, master, moment, second, grad_vec, vec, vec_moment, vec_second, m_new, s_new, w_new, copy, vm, vs, vw
+):
+    ff = master.shape[1] - KV_END
+    share = (D + ff) // 4
+    joined = join_columns((grad[0].astype(F32), grad[1].astype(F32)), ff, share)
+    first, new_second, weights = adam_update(
+        master[...], moment[...], second[...], joined, matrix_rate, weight_decay
+    )
+    m_new[...] = first
+    s_new[...] = new_second
+    w_new[...] = weights
+    copy[...] = weights.astype(BF16)
+
+    @pl.when(pl.program_id(0) == 0)
+    def _():
+        cores = [
+            jnp.concatenate([grad_vec[4 * core + row : 4 * core + row + 1, D:] for row in range(4)], axis=1)
+            for core in range(2)
+        ]
+        whole = jnp.concatenate(
+            [grad_vec[row : row + 1, :D] for row in range(5)] + [join_columns(cores, ff, share)], axis=1
+        )
+        vm[...], vs[...], vw[...] = adam_update(
+            vec[...], vec_moment[...], vec_second[...], whole, vector_rate, 0.0
+        )
+
+
+def adam_in(grad, master, moment, second, grad_vec, vec, vec_moment, vec_second):
+    rows, cols = master.shape
+    block = pl.BlockSpec((ADAM_ROWS, cols), lambda i: (i, 0))
+    still = pl.BlockSpec(vec.shape, lambda i: (0, 0))
+    shape = jax.ShapeDtypeStruct((rows, cols), F32)
+    vec_shape = jax.ShapeDtypeStruct(vec.shape, F32)
+    return pl.pallas_call(
+        adam_in_kernel,
+        grid=(rows // ADAM_ROWS,),
+        in_specs=[
+            pl.BlockSpec((2, ADAM_ROWS, grad.shape[2]), lambda i: (0, i, 0)),
+            block,
+            block,
+            block,
+            pl.BlockSpec(grad_vec.shape, lambda i: (0, 0)),
+            still,
+            still,
+            still,
+        ],
+        out_specs=[block] * 4 + [still] * 3,
+        out_shape=[shape] * 3 + [jax.ShapeDtypeStruct((rows, cols), BF16)] + [vec_shape] * 3,
+        compiler_params=pltpu.CompilerParams(vmem_limit_bytes=VMEM_LIMIT),
+        name="adam_in",
+    )(grad, master, moment, second, grad_vec, vec, vec_moment, vec_second)
+
+
+def adam_out_kernel(place_ref, grad, master, moment, second, m_new, s_new, w_new, copy):
+    first, new_second, weights = adam_update(
+        master[...], moment[...], second[...], grad[0].astype(F32), matrix_rate, weight_decay
+    )
+    m_new[...] = first
+    s_new[...] = new_second
+    w_new[...] = weights
+    copy[...] = weights.astype(BF16)
+
+
+def adam_out(places_of, grad, master, moment, second):
+    rows, cols = master.shape
+    count = rows // ADAM_OUT_ROWS
+    per_core = count // 2
+    block = pl.BlockSpec((ADAM_OUT_ROWS, cols), lambda i, table: (table[i], 0))
+    shape = jax.ShapeDtypeStruct((rows, cols), F32)
+    return pl.pallas_call(
+        adam_out_kernel,
+        grid_spec=pltpu.PrefetchScalarGridSpec(
+            num_scalar_prefetch=1,
+            grid=(count,),
+            in_specs=[
+                pl.BlockSpec(
+                    (1, ADAM_OUT_ROWS, cols), lambda i, table: (i // per_core, lax.rem(i, per_core), 0)
+                ),
+                block,
+                block,
+                block,
+            ],
+            out_specs=[block] * 4,
+        ),
+        out_shape=[shape] * 3 + [jax.ShapeDtypeStruct((rows, cols), BF16)],
+        compiler_params=pltpu.CompilerParams(vmem_limit_bytes=VMEM_LIMIT),
+        name="adam_out",
+    )(places_of, grad, master, moment, second)
 
 
 def fast_shards(
@@ -1284,96 +1448,42 @@
     rotary_scale,
 ):
     z = lax.axis_index("head")
-    c = lax.axis_index("ctx")
-    first_core = c == 0
-    rows = tokens.shape[0]
-    chip_rows = 2 * rows
+    chip_rows = 2 * tokens.shape[0]
     row_share = out_master.shape[0]
-    ff = in_master.shape[1] - KV_END
-    half_share = row_share // 2
-    attn_share = D // 2
-
-    def pick(array):
-        return jnp.where(
-            first_core, core_columns(array, 0, ff, row_share), core_columns(array, 1, ff, row_share)
-        )
-
-    win = pick(in_master.astype(BF16))
-    out_low = out_master.astype(BF16)
-    start_one = jnp.where(z == 0, attn_share * c, half_share * c)
-    start_two = jnp.where(z == 0, D + (half_share - attn_share) * c, half_share * c + attn_share)
-    wout = jnp.concatenate(
-        [
-            lax.dynamic_slice_in_dim(out_low, start_one, attn_share, 0),
-            lax.dynamic_slice_in_dim(out_low, start_two, half_share - attn_share, 0),
-        ],
-        axis=0,
-    )
-    bias = pick(vec_master[5 * D :])
-    attn_cols = HALF_D + 2 * HEAD_DIM
-    positions = z * chip_rows + jnp.arange(chip_rows, dtype=jnp.int32)
-    cosine, sine_table = rotary_tables(positions.astype(F32), rotary_scale[0].astype(F32))
-    affine = vec_master[: 4 * D].reshape(4, D)
-    cos_t, sin_t = cosine.T, sine_table.T
+    size = vec_master.shape[0]
+    vec, moments, seconds = (array.reshape(1, size) for array in (vec_master, vec_moment, vec_second))
+    positions = (z * chip_rows + jnp.arange(chip_rows, dtype=jnp.int32)).astype(F32)
+    cosine, sine_table = rotary_tables(positions, rotary_scale[0].astype(F32))
+    cosine, sine_table = cosine.T, sine_table.T
     full_in, full_out, all_tok, all_cot, norm_one, norm_two, att_t, dq_t, dkv = front(
-        win,
-        wout,
-        tokens,
-        cotangent,
-        affine,
-        bias[:attn_cols].reshape(1, attn_cols),
-        cos_t,
-        sin_t,
+        in_master, out_master, tokens, cotangent, vec, cosine, sine_table
     )
     output, input_grad, sum_in, sum_out, sum_vec = back(
-        full_in,
-        full_out,
-        all_tok,
-        all_cot,
-        norm_one,
-        norm_two,
-        att_t,
-        dq_t,
-        dkv,
-        affine,
-        bias[attn_cols:].reshape(1, -1),
-        vec_master[4 * D : 5 * D].reshape(1, D),
-        cos_t,
-        sin_t,
-    )
-    core_sums = sum_vec[:, D:].reshape(2, -1)
-    summed_vec = jnp.concatenate(
-        [sum_vec[:5, :D].reshape(-1), join_columns((core_sums[0], core_sums[1]), ff, row_share)]
-    )
-    sum_in = sum_in.reshape(2, -1, sum_in.shape[-1])
-    summed_in = join_columns((sum_in[0], sum_in[1]), ff, row_share).astype(F32)
-    low, high = sum_out.reshape(2, half_share, D)
-    head_rows = jnp.concatenate([low[:attn_share], high[:attn_share], low[attn_share:], high[attn_share:]], axis=0)
-    summed_out = jnp.where(z == 0, head_rows, jnp.concatenate([low, high], axis=0)).astype(F32)
-
-    in_moment_new, in_second_new, in_master_new = adam_update(
-        in_master, in_moment, in_second, summed_in, matrix_rate, weight_decay
-    )
-    out_moment_new, out_second_new, out_master_new = adam_update(
-        out_master, out_moment, out_second, summed_out, matrix_rate, weight_decay
-    )
-    vec_moment_new, vec_second_new, vec_master_new = adam_update(
-        vec_master, vec_moment, vec_second, summed_vec, vector_rate, 0.0
+        full_in, full_out, all_tok, all_cot, norm_one, norm_two, att_t, dq_t, dkv, vec, cosine, sine_table
+    )
+    count = row_share // ADAM_OUT_ROWS
+    half, attn = count // 2, HALF_D // ADAM_OUT_ROWS
+    plain = jnp.arange(count, dtype=jnp.int32)
+    core, place = plain // half, plain % half
+    first_owner = jnp.where(place < attn, core * attn + place, 2 * attn + core * (half - attn) + place - attn)
+    table = jnp.where(z == 0, first_owner, plain)
+    out_new = adam_out(table, sum_out.reshape(2, -1, D), out_master, out_moment, out_second)
+    in_new = adam_in(
+        sum_in.reshape(2, -1, sum_in.shape[-1]),
+        in_master,
+        in_moment,
+        in_second,
+        sum_vec,
+        vec,
+        moments,
+        seconds,
     )
     return (
         output,
         input_grad,
-        in_moment_new,
-        in_second_new,
-        in_master_new,
-        in_master_new.astype(BF16),
-        out_moment_new,
-        out_second_new,
-        out_master_new,
-        out_master_new.astype(BF16),
-        vec_moment_new,
-        vec_second_new,
-        vec_master_new,
+        *in_new[:4],
+        *out_new,
+        *(array.reshape(size) for array in in_new[4:]),
     )
 
 

time: 231 us -> 198 us (0.86)
  local copies, waits for them, and re-layouts: 27.2 us -> 4.93 us
  other arithmetic: 19.1 us -> 3.36 us
  Pallas kernels: 182 us -> 187 us
    pallas_call x1 -> x3, Pallas kernels: 70.9 us -> 88.9 us  [the longest x1 66.7 us: front(): pl.pallas_call(front_kernel, out_shape=(jax.ShapeDtypeStruct((4 * in_mast...]
    convert_element_type x4 -> x0, other arithmetic: 15 us -> none  [the longest x1 8.04 us: fast_shards(): out_master_new.astype(BF16)]
    slice x30 -> x0, local copies, waits for them, and re-layouts: 13.8 us -> none  [the longest x4 2.28 us: join_columns(): pieces += [pair[0][..., at:at + size], pair[1][..., at:at + size]]]
    pallas_call x1, Pallas kernels: 111 us -> 98.4 us  [back(): pl.pallas_call(back_kernel, out_shape=(jax.ShapeDtypeStruct((rows, D), BF...]
    concatenate x6 -> x0, local copies, waits for them, and re-layouts: 5.61 us -> none  [the longest x1 4.1 us: join_columns(): return jnp.concatenate(pieces, axis=-1)]
    unnamed x29 -> x14, local copies, waits for them, and re-layouts: 4.37 us -> 1.52 us
where the time goes in v1:
time: 198 us; the launch traced here: 197 us
  Pallas kernels  187 us (94%)
  local copies, waits for them, and re-layouts  4.93 us (2%)
  other arithmetic  3.36 us (2%)
    pallas_call x1, Pallas kernels, back(): pl.pallas_call(back_kernel, out_shape=(jax.ShapeDtypeStruct((rows, D), BF...  98.4 us
    pallas_call x1, Pallas kernels, front(): pl.pallas_call(front_kernel, out_shape=(jax.ShapeDtypeStruct((4 * in_mast...  66.7 us
    pallas_call x1, Pallas kernels, adam_out(): pl.pallas_call(adam_out_kernel, grid_spec=pltpu.PrefetchScalarGridSpec(nu...  12 us
    pallas_call x1, Pallas kernels, adam_in(): pl.pallas_call(adam_in_kernel, grid=(rows // ADAM_ROWS,), in_specs=[pl.Bl...  10.2 us

profile of v1, /device:TPU:0, one launch (start us, length us, event | category | flops | bytes accessed | tf_op | source)
XLA Modules:
  0.0 197.0 jit_solution(15672543896163789090)
XLA Ops:
  0.6 1.4 reshape.64.vec.vec_ref
  2.7 0.8 multiply_sine_fusion
  3.5 66.7 %front.1 = (bf16[768,2048]{1,0:T(8,128)(2,1)}, bf16[1920,768]{1,0:T(8,128)(2,1)}, bf16[2,256,768]{2,1,0:T(8,128)(2,1)}, bf16[2,256,768]{2,1,0:T(8,128)(2,1)}, bf...) custom-call(f32[192,3968]{1,0:T(8,128)} %master.2, ...), custom_call_target="tpu_custom_call" | custom-call | tf_op jit(solution)/shard_map/front/pallas_call | solution.py:816
  70.2 0.0 copy-start.2
  70.2 98.4 %back.1 = (bf16[256,768]{1,0:T(8,128)(2,1)}, bf16[256,768]{1,0:T(8,128)(2,1)}, bf16[2,4,48,2048]{3,2,1,0:T(8,128)(2,1)}, bf16[2,4,120,768]{3,2,1,0:T(8,128)(2,1)}, f32[8,1280]{1,0:T(8,128)}) custom-call(bf16[768,2048]{1,0:T(8,128)(2,1)} %get-tuple-element.38.full_in, bf16[1920,768]{1,0:T(8,128)(2,1)} %get-tuple-element.39.full_out, ...), custom_call_target="tpu_custom_call" | custom-call | tf_op jit(solution)/shard_map/back/pallas_call | solution.py:1289
  168.6 0.0 copy-done.2
  168.6 0.6 reshape.66.vec_moment
  169.3 1.4 reshape.67.vec_second
  170.7 10.2 %adam_in.1 = (f32[192,3968]{1,0:T(8,128)}, f32[192,3968]{1,0:T(8,128)}, f32[192,3968]{1,0:T(8,128)}, bf16[192,3968]{1,0:T(8,128)(2,1)}, f32[1,7808]{1,0:T(1,128)}, /*index=5*/f32[1,7808]{1,0:T(1,128)}, f32[1,7808]{1,0:T(1,128)}) custom-call(bf16[2,192,2048]{2,1,0:T(8,128)(2,1)} %bitcast.3, f32[192,3968]{1,0:T(8,128)} %master.2, f32[192,3968]{1,0:T(8,128)} %moment.2, ...), custom_call_target="tpu_custom_call" | custom-call | tf_op jit(solution)/shard_map/adam_in/pallas_call | solution.py:1379
  180.9 0.5 broadcast_select_fusion.place_ref
  181.4 0.0 copy-start.5
  181.4 0.0 copy-start.4
  181.4 0.0 copy-start.3
  181.4 0.0 copy-start.1
  181.4 0.0 copy-start
  181.4 12.0 %adam_out.1 = (f32[960,768]{1,0:T(8,128)}, f32[960,768]{1,0:T(8,128)}, f32[960,768]{1,0:T(8,128)}, bf16[960,768]{1,0:T(8,128)(2,1)}) custom-call(s32[10]{0:T(128)} %broadcast_select_fusion.place_ref, bf16[2,480,768]{2,1,0:T(8,128)(2,1)} %bitcast.4, f32[960,768]{1,0:T(8,128)} %master.3, f32[960,768]{1,0:T(8,128)} %moment.3, f32[960,768]{1,0:T(8,128)} %second.3), custom_call_target="tpu_custom_call" | custom-call | tf_op jit(solution)/shard_map/adam_out/pallas_call | solution.py:1415
  193.4 0.0 copy-done.5
  193.4 0.7 reduce
  194.1 0.0 copy-done.4
  194.1 0.7 reduce.1
  194.8 0.0 copy-done.3
  194.8 0.7 reduce.2
  195.5 0.0 copy-done.1
  195.5 0.7 copy.28
  196.2 0.0 copy-done
  196.2 0.7 copy.29
  (2 shorter events, 0.0 us)
Async XLA Ops:
  70.2 98.4 %copy-start.2 = (f32[7808]{0:T(1024)S(1)}, f32[7808]{0:T(1024)}, u32[]{:S(2)}) copy-start(f32[7808]{0:T(1024)} %param.21) | copy-start | bytes 93700
  181.4 12.0 %copy-start.5 = (f32[1,7808]{1,0:T(1,128)S(1)}, f32[1,7808]{1,0:T(1,128)}, u32[]{:S(2)}) copy-start(f32[1,7808]{1,0:T(1,128)} %get-tuple-element.60) | copy-start | bytes 93700
  181.4 12.7 %copy-start.4 = (f32[1,7808]{1,0:T(1,128)S(1)}, f32[1,7808]{1,0:T(1,128)}, u32[]{:S(2)}) copy-start(f32[1,7808]{1,0:T(1,128)} %get-tuple-element.61) | copy-start | bytes 93700
  181.4 13.4 %copy-start.3 = (f32[1,7808]{1,0:T(1,128)S(1)}, f32[1,7808]{1,0:T(1,128)}, u32[]{:S(2)}) copy-start(f32[1,7808]{1,0:T(1,128)} %get-tuple-element.62) | copy-start | bytes 93700
  181.4 14.1 %copy-start.1 = (bf16[256,768]{1,0:T(8,128)(2,1)S(1)}, bf16[256,768]{1,0:T(8,128)(2,1)}, u32[]{:S(2)}) copy-start(bf16[256,768]{1,0:T(8,128)(2,1)} %get-tuple-element.78) | copy-start | bytes 1179652
  181.4 14.8 %copy-start = (bf16[256,768]{1,0:T(8,128)(2,1)S(1)}, bf16[256,768]{1,0:T(8,128)(2,1)}, u32[]{:S(2)}) copy-start(bf16[256,768]{1,0:T(8,128)(2,1)} %get-tuple-element.79) | copy-start | bytes 1179652

commit v2 on v1

--- a/solution.py
+++ b/solution.py
@@ -332,8 +332,9 @@
 F32 = jnp.float32
 BF16 = jnp.bfloat16
 HALF_HEADS = HEADS // 2
-VMEM_LIMIT = 60 * 1024 * 1024
-BACK_LIMIT = 67000000
+VMEM_LIMIT = 30 * 1024 * 1024
+ADAM_LIMIT = 47 * 1024 * 1024
+BACK_LIMIT = 38 * 1024 * 1024
 
 
 def vmem_specs(count):
@@ -405,10 +406,20 @@
 OUT_ROWS = 120
 
 
+LANES = 128
+
+
+def vec_row(vec, first, last):
+    return jnp.concatenate(
+        [vec[row : row + 1, :] for row in range(first // LANES, last // LANES)], axis=1
+    )
+
+
 def core_bias(vec, c, first, last):
-    ff = vec.shape[1] - 5 * D - KV_END
+    size = vec.shape[0] * LANES
+    ff = size - 5 * D - KV_END
     share = (D + ff) // 4
-    tail = vec[:, 5 * D :]
+    tail = vec_row(vec, 5 * D, size)
     return jnp.where(
         c == 0, core_columns(tail, 0, ff, share), core_columns(tail, 1, ff, share)
     )[:, first:last]
@@ -438,6 +449,9 @@
     values,
     weights,
     tops,
+    kept_out,
+    kept_top,
+    kept_inverse,
     dkeys,
     dvalues,
     z_send,
@@ -594,8 +608,10 @@
         inverse = lax.rsqrt(jnp.mean(center * center, axis=-1, keepdims=True) + 1e-05)
         normed = center * inverse
         here = pl.ds(pl.multiple_of(half * rows, rows), rows)
-        norm_one[here, :] = (normed * vec[:, :D] + vec[:, D : 2 * D]).astype(BF16)
-        norm_two[here, :] = (normed * vec[:, 2 * D : 3 * D] + vec[:, 3 * D : 4 * D]).astype(BF16)
+        norm_one[here, :] = (normed * vec_row(vec, 0, D) + vec_row(vec, D, 2 * D)).astype(BF16)
+        norm_two[here, :] = (
+            normed * vec_row(vec, 2 * D, 3 * D) + vec_row(vec, 3 * D, 4 * D)
+        ).astype(BF16)
 
     for copy in locals_:
         copy.wait()
@@ -672,9 +688,10 @@
         (0, 0, 0): ((spread, 1, 3),),
         (0, 0, 1): ((relay, 1, 2),),
         (0, 0, 3): ((spread, 2, 1),),
-        (0, 1, 0): ((spread, 2, 2),),
-        (0, 1, 2): ((relay, 2, 1), (spread, 2, 3)),
-        (1, 0, 1): ((relay, 2, 2),),
+        (1, 0, 0): ((relay, 1, 3),),
+        (1, 0, 1): ((spread, 2, 2),),
+        (1, 0, 3): ((relay, 2, 1), (spread, 2, 3)),
+        (0, 1, 1): ((relay, 2, 2),),
         (1, 1, 0): ((relay, 2, 3),),
     }
 
@@ -688,7 +705,6 @@
                         action(group, far)
 
     def upstream_heads():
-        relay(1, 3)
         settle(1)
         for head in range(HALF_HEADS):
             part = full_out[pl.ds(head * HEAD_DIM, HEAD_DIM), :]
@@ -697,12 +713,12 @@
                     part, all_cot[half], contract_cols, preferred_element_type=F32
                 ).astype(BF16)
 
-    def two_heads(pair, carry):
+    def rows_at(index):
+        return pl.ds(pl.multiple_of(index * CHUNK, CHUNK), CHUNK)
+
+    def forward_pair(pair, slot):
         cols = pl.ds(pl.multiple_of(pair * width, width), width)
         queries = q_all[:, cols]
-
-        def rows_at(index):
-            return pl.ds(pl.multiple_of(index * CHUNK, CHUNK), CHUNK)
 
         def forward(index, state, diagonal):
             top, total, out = state
@@ -714,8 +730,8 @@
             above = jnp.maximum(top, jnp.max(part, axis=0, keepdims=True))
             part = jnp.exp(part - above)
             rounded = part.astype(BF16)
-            weights[rows_at(index), :] = rounded
-            tops[index] = above
+            weights[slot, rows_at(index), :] = rounded
+            tops[slot, index] = above
             scale = jnp.exp(top - above)
             total = total * scale + jnp.sum(part, axis=0, keepdims=True)
             out = out * scale + jnp.dot(
@@ -743,16 +759,23 @@
         second = pl.multiple_of(base + HEAD_DIM, HEAD_DIM)
         att_ref[pl.ds(base, HEAD_DIM), :] = out[:, :CHUNK].astype(BF16)
         att_ref[pl.ds(second, HEAD_DIM), :] = out[:, CHUNK:].astype(BF16)
-        pl.when(pair == 0)(upstream_heads)
+        kept_out[slot] = out
+        kept_top[slot] = top
+        kept_inverse[slot] = inverse
+
+    def backward_pair(pair, slot):
+        cols = pl.ds(pl.multiple_of(pair * width, width), width)
+        queries = q_all[:, cols]
         grads = g_all[:, cols].astype(F32)
-        inner = jnp.sum(grads * out, axis=0, keepdims=True)
+        top, inverse = kept_top[slot], kept_inverse[slot]
+        inner = jnp.sum(grads * kept_out[slot], axis=0, keepdims=True)
 
         def backward(index, dq):
             here = rows_at(index)
-            factor = inverse * jnp.exp(tops[index] - top)
+            factor = inverse * jnp.exp(tops[slot, index] - top)
             scaled = (grads * factor).astype(BF16)
             dprob = jnp.dot(values[here, :], scaled, preferred_element_type=F32)
-            rounded = weights[here, :]
+            rounded = weights[slot, here, :]
             dscore = (rounded.astype(F32) * (dprob - inner * factor)).astype(BF16)
             dkeys[here, :] += lax.dot_general(
                 dscore, queries, contract_cols, preferred_element_type=F32
@@ -768,11 +791,29 @@
 
         dq = lax.fori_loop(0, 4, backward_or_not, jnp.zeros((HEAD_DIM, width), F32))
         dq = turn(dq * 0.125, cos_two, -sin_two)
+        base = pl.multiple_of(pair * 2 * HEAD_DIM, 2 * HEAD_DIM)
+        second = pl.multiple_of(base + HEAD_DIM, HEAD_DIM)
         dq_ref[pl.ds(base, HEAD_DIM), :] = dq[:, :CHUNK].astype(BF16)
         dq_ref[pl.ds(second, HEAD_DIM), :] = dq[:, CHUNK:].astype(BF16)
+
+    def phase(step, carry):
+        pair = jnp.where(step < 4, lax.rem(step, 2), 2)
+        slot = lax.rem(pair, 2)
+        ahead = jnp.logical_or(step < 2, step == 4)
+
+        @pl.when(ahead)
+        def _():
+            forward_pair(pair, slot)
+
+        pl.when(step == 1)(upstream_heads)
+
+        @pl.when(jnp.logical_not(ahead))
+        def _():
+            backward_pair(pair, slot)
+
         return carry
 
-    lax.fori_loop(0, HALF_HEADS // 2, two_heads, 0)
+    lax.fori_loop(0, 6, phase, 0)
 
     for index in range(4):
         here = pl.ds(index * CHUNK, CHUNK)
@@ -834,8 +875,11 @@
             pltpu.VMEM((4, 2 * HEAD_DIM, CHUNK), BF16),
             pltpu.VMEM((4 * CHUNK, HEAD_DIM), BF16),
             pltpu.VMEM((4 * CHUNK, HEAD_DIM), BF16),
-            pltpu.VMEM((4 * CHUNK, 2 * CHUNK), BF16),
-            pltpu.VMEM((4, 1, 2 * CHUNK), F32),
+            pltpu.VMEM((2, 4 * CHUNK, 2 * CHUNK), BF16),
+            pltpu.VMEM((2, 4, 1, 2 * CHUNK), F32),
+            pltpu.VMEM((2, HEAD_DIM, 2 * CHUNK), F32),
+            pltpu.VMEM((2, 1, 2 * CHUNK), F32),
+            pltpu.VMEM((2, 1, 2 * CHUNK), F32),
             pltpu.VMEM((4 * CHUNK, HEAD_DIM), F32),
             pltpu.VMEM((4 * CHUNK, HEAD_DIM), F32),
             dma((3, 4, 2)),
@@ -882,7 +926,6 @@
     one_t,
     two_t,
     act,
-    slope,
     dhid,
     branch_t,
     qkv_grad,
@@ -1087,9 +1130,9 @@
 
     branch_t[pl.ds(0, HALF_D), :] = att_ref[...]
     bias_up = core_bias(vec_ref, c, attn_cols, attn_cols + hidden)
-    for number in range(hidden // HIDDEN_BLOCK):
-        cols = pl.ds(number * HIDDEN_BLOCK, HIDDEN_BLOCK)
-        before = (
+
+    def before_gelu(number):
+        return (
             jnp.dot(
                 norm_two[...],
                 full_in[:, pl.ds(attn_cols + number * HIDDEN_BLOCK, HIDDEN_BLOCK)],
@@ -1097,10 +1140,11 @@
             )
             + bias_up[:, number * HIDDEN_BLOCK : (number + 1) * HIDDEN_BLOCK]
         )
-        normal = 0.5 * (1.0 + lax.erf(before * ROOT_HALF))
-        active = before * normal
-        act[:, cols] = active.astype(BF16)
-        slope[:, cols] = normal + before * (GAUSS * jnp.exp(-0.5 * before * before))
+
+    for number in range(hidden // HIDDEN_BLOCK):
+        before = before_gelu(number)
+        active = 0.5 * before * (1.0 + lax.erf(before * ROOT_HALF))
+        act[:, pl.ds(number * HIDDEN_BLOCK, HIDDEN_BLOCK)] = active.astype(BF16)
         branch_t[pl.ds(HALF_D + number * HIDDEN_BLOCK, HIDDEN_BLOCK), :] = active.T.astype(BF16)
     exchange(0)
     exchange(1)
@@ -1117,6 +1161,10 @@
     two_t[...] = norm_two[...].astype(F32).T.astype(BF16)
     for number in range(hidden // HIDDEN_BLOCK):
         cols = pl.ds(number * HIDDEN_BLOCK, HIDDEN_BLOCK)
+        before = before_gelu(number)
+        slope = 0.5 * (1.0 + lax.erf(before * ROOT_HALF)) + before * (
+            GAUSS * jnp.exp(-0.5 * before * before)
+        )
         for k in range(2):
             here = pl.ds(k * rows, rows)
             back = lax.dot_general(
@@ -1125,7 +1173,7 @@
                 contract_cols,
                 preferred_element_type=F32,
             )
-            dhid[here, cols] = (back * slope[here, cols]).astype(BF16)
+            dhid[here, cols] = (back * slope[k * rows : (k + 1) * rows, :]).astype(BF16)
     halve(0)
     exchange(2)
     dkv[mine, :] = summed[z]
@@ -1171,6 +1219,7 @@
     once = jnp.where(column < HALF_D, 1.0, keep)
     first_rows = jnp.zeros((1, D), F32)
     sums = [first_rows] * 4
+    gain_one, gain_two = vec_row(vec_ref, 0, D), vec_row(vec_ref, 2 * D, 3 * D)
     for k in range(2):
         here = pl.ds(k * rows, rows)
         inputs = all_tok[k].astype(F32)
@@ -1189,7 +1238,7 @@
         )
         terms = (one * normed, one, two * normed, two)
         sums = [old + jnp.sum(term, axis=0, keepdims=True) for old, term in zip(sums, terms)]
-        upstream[here, :] = one * vec_ref[:, :D] + two * vec_ref[:, 2 * D : 3 * D]
+        upstream[here, :] = one * gain_one + two * gain_two
     send(upstream.at[other, :], up_other, parts, 3, to_pair)
     halve(3)
     exchange(5)
@@ -1235,7 +1284,7 @@
     close(1)
     landed(out_other, parts, 2)
     output_ref[...] = (
-        all_tok[c].astype(F32) + (partial_out[mine, :] + out_other[...]) + vec_ref[:, 4 * D : 5 * D]
+        all_tok[c].astype(F32) + (partial_out[mine, :] + out_other[...]) + vec_row(vec_ref, 4 * D, 5 * D)
     ).astype(BF16)
     landed(up_other, parts, 3)
     inputs = all_tok[c].astype(F32)
@@ -1301,7 +1350,6 @@
             pltpu.VMEM((D, chip_rows), BF16),
             pltpu.VMEM((D, chip_rows), BF16),
             pltpu.VMEM((chip_rows, hidden), BF16),
-            pltpu.VMEM((chip_rows, hidden), F32),
             pltpu.VMEM((chip_rows, hidden), BF16),
             pltpu.VMEM((HALF_D + hidden, chip_rows), BF16),
             pltpu.VMEM((chip_rows, HALF_D + kv_width), BF16),
@@ -1342,95 +1390,210 @@
 ADAM_OUT_ROWS = 96
 
 
-def adam_in_kernel(
-    grad, master, moment, second, grad_vec, vec, vec_moment, vec_second, m_new, s_new, w_new, copy, vm, vs, vw
+def adam_fast(master, moment, second, gradient, step_rate, decay_rate):
+    moment_new = 0.5 * moment + 0.5 * gradient
+    second_new = 0.5 * second + 0.5 * gradient * gradient
+    scale = 1.0 / (1.0 - 0.5**ADAM_STEP)
+    normalized = moment_new * scale / (jnp.sqrt(second_new * scale) + adam_epsilon)
+    return moment_new, second_new, master - step_rate * (normalized + decay_rate * master)
+
+
+def adam_kernel(
+    grad_in,
+    grad_out,
+    in_master,
+    in_moment,
+    in_second,
+    out_master,
+    out_moment,
+    out_second,
+    grad_vec,
+    vec,
+    vec_moment,
+    vec_second,
+    in_m,
+    in_s,
+    in_w,
+    in_c,
+    out_m,
+    out_s,
+    out_w,
+    out_c,
+    vec_m,
+    vec_s,
+    vec_w,
+    held_gi,
+    held_go,
+    held_in,
+    held_out,
+    low_in,
+    low_out,
+    load_in,
+    load_out,
+    store_in,
+    store_out,
 ):
-    ff = master.shape[1] - KV_END
-    share = (D + ff) // 4
-    joined = join_columns((grad[0].astype(F32), grad[1].astype(F32)), ff, share)
-    first, new_second, weights = adam_update(
-        master[...], moment[...], second[...], joined, matrix_rate, weight_decay
-    )
-    m_new[...] = first
-    s_new[...] = new_second
-    w_new[...] = weights
-    copy[...] = weights.astype(BF16)
-
-    @pl.when(pl.program_id(0) == 0)
-    def _():
-        cores = [
-            jnp.concatenate([grad_vec[4 * core + row : 4 * core + row + 1, D:] for row in range(4)], axis=1)
-            for core in range(2)
+    z = lax.axis_index("head")
+    rows_in, cols_in = in_master.shape
+    rows_out = out_master.shape[0]
+    ff = cols_in - KV_END
+    count_in, count_out = rows_in // ADAM_ROWS, rows_out // ADAM_OUT_ROWS
+    half, attn = count_out // 2, HALF_D // ADAM_OUT_ROWS
+
+    def in_rows(number):
+        return pl.ds(pl.multiple_of(number * ADAM_ROWS, ADAM_ROWS), ADAM_ROWS)
+
+    def out_rows(number):
+        core, place = number // half, lax.rem(number, half)
+        first = jnp.where(
+            place < attn, core * attn + place, 2 * attn + core * (half - attn) + place - attn
+        )
+        block = jnp.where(z == 0, first, number)
+        return pl.ds(pl.multiple_of(block * ADAM_OUT_ROWS, 8), ADAM_OUT_ROWS)
+
+    def loads_in(number):
+        here = in_rows(number)
+        copies = [
+            pltpu.make_async_copy(ref.at[here, :], held_in.at[k, here, :], load_in.at[number, k])
+            for k, ref in enumerate((in_master, in_moment, in_second))
         ]
-        whole = jnp.concatenate(
-            [grad_vec[row : row + 1, :D] for row in range(5)] + [join_columns(cores, ff, share)], axis=1
-        )
-        vm[...], vs[...], vw[...] = adam_update(
-            vec[...], vec_moment[...], vec_second[...], whole, vector_rate, 0.0
-        )
-
-
-def adam_in(grad, master, moment, second, grad_vec, vec, vec_moment, vec_second):
-    rows, cols = master.shape
-    block = pl.BlockSpec((ADAM_ROWS, cols), lambda i: (i, 0))
-    still = pl.BlockSpec(vec.shape, lambda i: (0, 0))
-    shape = jax.ShapeDtypeStruct((rows, cols), F32)
-    vec_shape = jax.ShapeDtypeStruct(vec.shape, F32)
+        return copies + [
+            pltpu.make_async_copy(grad_in.at[:, here, :], held_gi.at[:, here, :], load_in.at[number, 3])
+        ]
+
+    def loads_out(number):
+        here = out_rows(number)
+        core, place = number // half, lax.rem(number, half)
+        rows = pl.ds(pl.multiple_of(place * ADAM_OUT_ROWS, 16), ADAM_OUT_ROWS)
+        copies = [
+            pltpu.make_async_copy(ref.at[here, :], held_out.at[k, number], load_out.at[number, k])
+            for k, ref in enumerate((out_master, out_moment, out_second))
+        ]
+        return copies + [
+            pltpu.make_async_copy(grad_out.at[core, rows, :], held_go.at[number], load_out.at[number, 3])
+        ]
+
+    def stores_in(number):
+        here = in_rows(number)
+        copies = [
+            pltpu.make_async_copy(held_in.at[k, here, :], ref.at[here, :], store_in.at[number, k])
+            for k, ref in enumerate((in_w, in_m, in_s))
+        ]
+        return copies + [
+            pltpu.make_async_copy(low_in.at[here, :], in_c.at[here, :], store_in.at[number, 3])
+        ]
+
+    def stores_out(number):
+        here = out_rows(number)
+        copies = [
+            pltpu.make_async_copy(held_out.at[k, number], ref.at[here, :], store_out.at[number, k])
+            for k, ref in enumerate((out_w, out_m, out_s))
+        ]
+        return copies + [
+            pltpu.make_async_copy(low_out.at[number], out_c.at[here, :], store_out.at[number, 3])
+        ]
+
+    def every(count, copies_of, start):
+        def one(number, carry):
+            for copy in copies_of(number):
+                copy.start() if start else copy.wait()
+            return carry
+
+        lax.fori_loop(0, count, one, 0)
+
+    every(count_out, loads_out, True)
+    every(count_in, loads_in, True)
+
+    def step_out(number, carry):
+        for copy in loads_out(number):
+            copy.wait()
+        first, new_second, weights = adam_fast(
+            held_out[0, number],
+            held_out[1, number],
+            held_out[2, number],
+            held_go[number].astype(F32),
+            matrix_rate,
+            weight_decay,
+        )
+        held_out[0, number] = weights
+        held_out[1, number] = first
+        held_out[2, number] = new_second
+        low_out[number] = weights.astype(BF16)
+        for copy in stores_out(number):
+            copy.start()
+        return carry
+
+    lax.fori_loop(0, count_out, step_out, 0)
+
+    def step_in(number, carry):
+        for copy in loads_in(number):
+            copy.wait()
+        here = in_rows(number)
+        joined = join_columns(
+            (held_gi[0, here, :].astype(F32), held_gi[1, here, :].astype(F32)), ff, rows_out
+        )
+        first, new_second, weights = adam_fast(
+            held_in[0, here, :], held_in[1, here, :], held_in[2, here, :], joined, matrix_rate, weight_decay
+        )
+        held_in[0, here, :] = weights
+        held_in[1, here, :] = first
+        held_in[2, here, :] = new_second
+        low_in[here, :] = weights.astype(BF16)
+        for copy in stores_in(number):
+            copy.start()
+        return carry
+
+    lax.fori_loop(0, count_in, step_in, 0)
+    cores = [
+        jnp.concatenate([grad_vec[4 * core + row : 4 * core + row + 1, D:] for row in range(4)], axis=1)
+        for core in range(2)
+    ]
+    whole = jnp.concatenate(
+        [grad_vec[row : row + 1, :D] for row in range(5)] + [join_columns(cores, ff, rows_out)], axis=1
+    )
+    size = whole.shape[1]
+    results = adam_fast(
+        vec_row(vec, 0, size), vec_row(vec_moment, 0, size), vec_row(vec_second, 0, size), whole, vector_rate, 0.0
+    )
+    for target, result in zip((vec_m, vec_s, vec_w), results):
+        for row in range(size // LANES):
+            target[row : row + 1, :] = result[:, row * LANES : (row + 1) * LANES]
+    every(count_out, stores_out, False)
+    every(count_in, stores_in, False)
+
+
+def adam(grad_in, grad_out, in_arrays, out_arrays, grad_vec, vec_arrays):
+    rows_in, cols_in = in_arrays[0].shape
+    rows_out, cols_out = out_arrays[0].shape
+    count_in, count_out = rows_in // ADAM_ROWS, rows_out // ADAM_OUT_ROWS
+    anywhere = pl.BlockSpec(memory_space=pl.ANY)
+    still = pl.BlockSpec(memory_space=pltpu.VMEM)
+    dma = pltpu.SemaphoreType.DMA
+
+    def shapes(array, low):
+        whole = jax.ShapeDtypeStruct(array.shape, F32)
+        return [whole] * 3 + ([jax.ShapeDtypeStruct(array.shape, BF16)] if low else [])
+
     return pl.pallas_call(
-        adam_in_kernel,
-        grid=(rows // ADAM_ROWS,),
-        in_specs=[
-            pl.BlockSpec((2, ADAM_ROWS, grad.shape[2]), lambda i: (0, i, 0)),
-            block,
-            block,
-            block,
-            pl.BlockSpec(grad_vec.shape, lambda i: (0, 0)),
-            still,
-            still,
-            still,
+        adam_kernel,
+        out_shape=shapes(in_arrays[0], True) + shapes(out_arrays[0], True) + shapes(vec_arrays[0], False),
+        in_specs=[anywhere] * 8 + [still] * 4,
+        out_specs=[anywhere] * 8 + [still] * 3,
+        scratch_shapes=[
+            pltpu.VMEM(grad_in.shape, BF16),
+            pltpu.VMEM((count_out, ADAM_OUT_ROWS, cols_out), BF16),
+            pltpu.VMEM((3, rows_in, cols_in), F32),
+            pltpu.VMEM((3, count_out, ADAM_OUT_ROWS, cols_out), F32),
+            pltpu.VMEM((rows_in, cols_in), BF16),
+            pltpu.VMEM((count_out, ADAM_OUT_ROWS, cols_out), BF16),
+            dma((count_in, 4)),
+            dma((count_out, 4)),
+            dma((count_in, 4)),
+            dma((count_out, 4)),
         ],
-        out_specs=[block] * 4 + [still] * 3,
-        out_shape=[shape] * 3 + [jax.ShapeDtypeStruct((rows, cols), BF16)] + [vec_shape] * 3,
-        compiler_params=pltpu.CompilerParams(vmem_limit_bytes=VMEM_LIMIT),
-        name="adam_in",
-    )(grad, master, moment, second, grad_vec, vec, vec_moment, vec_second)
-
-
-def adam_out_kernel(place_ref, grad, master, moment, second, m_new, s_new, w_new, copy):
-    first, new_second, weights = adam_update(
-        master[...], moment[...], second[...], grad[0].astype(F32), matrix_rate, weight_decay
-    )
-    m_new[...] = first
-    s_new[...] = new_second
-    w_new[...] = weights
-    copy[...] = weights.astype(BF16)
-
-
-def adam_out(places_of, grad, master, moment, second):
-    rows, cols = master.shape
-    count = rows // ADAM_OUT_ROWS
-    per_core = count // 2
-    block = pl.BlockSpec((ADAM_OUT_ROWS, cols), lambda i, table: (table[i], 0))
-    shape = jax.ShapeDtypeStruct((rows, cols), F32)
-    return pl.pallas_call(
-        adam_out_kernel,
-        grid_spec=pltpu.PrefetchScalarGridSpec(
-            num_scalar_prefetch=1,
-            grid=(count,),
-            in_specs=[
-                pl.BlockSpec(
-                    (1, ADAM_OUT_ROWS, cols), lambda i, table: (i // per_core, lax.rem(i, per_core), 0)
-                ),
-                block,
-                block,
-                block,
-            ],
-            out_specs=[block] * 4,
-        ),
-        out_shape=[shape] * 3 + [jax.ShapeDtypeStruct((rows, cols), BF16)],
-        compiler_params=pltpu.CompilerParams(vmem_limit_bytes=VMEM_LIMIT),
-        name="adam_out",
-    )(places_of, grad, master, moment, second)
+        compiler_params=pltpu.CompilerParams(vmem_limit_bytes=ADAM_LIMIT),
+        name="adam",
+    )(grad_in, grad_out, *in_arrays, *out_arrays, grad_vec, *vec_arrays)
 
 
 def fast_shards(
@@ -1449,9 +1612,10 @@
 ):
     z = lax.axis_index("head")
     chip_rows = 2 * tokens.shape[0]
-    row_share = out_master.shape[0]
     size = vec_master.shape[0]
-    vec, moments, seconds = (array.reshape(1, size) for array in (vec_master, vec_moment, vec_second))
+    vec, moments, seconds = (
+        array.reshape(-1, LANES) for array in (vec_master, vec_moment, vec_second)
+    )
     positions = (z * chip_rows + jnp.arange(chip_rows, dtype=jnp.int32)).astype(F32)
     cosine, sine_table = rotary_tables(positions, rotary_scale[0].astype(F32))
     cosine, sine_table = cosine.T, sine_table.T
@@ -1461,30 +1625,15 @@
     output, input_grad, sum_in, sum_out, sum_vec = back(
         full_in, full_out, all_tok, all_cot, norm_one, norm_two, att_t, dq_t, dkv, vec, cosine, sine_table
     )
-    count = row_share // ADAM_OUT_ROWS
-    half, attn = count // 2, HALF_D // ADAM_OUT_ROWS
-    plain = jnp.arange(count, dtype=jnp.int32)
-    core, place = plain // half, plain % half
-    first_owner = jnp.where(place < attn, core * attn + place, 2 * attn + core * (half - attn) + place - attn)
-    table = jnp.where(z == 0, first_owner, plain)
-    out_new = adam_out(table, sum_out.reshape(2, -1, D), out_master, out_moment, out_second)
-    in_new = adam_in(
+    updated = adam(
         sum_in.reshape(2, -1, sum_in.shape[-1]),
-        in_master,
-        in_moment,
-        in_second,
+        sum_out.reshape(2, -1, D),
+        (in_master, in_moment, in_second),
+        (out_master, out_moment, out_second),
         sum_vec,
-        vec,
-        moments,
-        seconds,
-    )
-    return (
-        output,
-        input_grad,
-        *in_new[:4],
-        *out_new,
-        *(array.reshape(size) for array in in_new[4:]),
-    )
+        (vec, moments, seconds),
+    )
+    return (output, input_grad, *updated[:8], *(array.reshape(size) for array in updated[8:]))
 
 
 def solution(mesh):

time: 198 us -> 178 us (0.90)
  Pallas kernels: 187 us -> 168 us
  other arithmetic: 3.36 us -> 0.16 us
  local copies, waits for them, and re-layouts: 4.93 us -> 7.95 us
    pallas_call x1, Pallas kernels: 66.7 us -> 59.4 us  [front(): pl.pallas_call(front_kernel, out_shape=(jax.ShapeDtypeStruct((4 * in_mast...]
    pallas_call x2 -> x1, Pallas kernels: 22.2 us -> 15.1 us  [adam(): pl.pallas_call(adam_kernel, out_shape=shapes(in_arrays[0], True) + shapes...]
    unnamed x14 -> x20, local copies, waits for them, and re-layouts: 1.52 us -> 7.95 us
    pallas_call x1, Pallas kernels: 98.4 us -> 93.4 us  [back(): pl.pallas_call(back_kernel, out_shape=(jax.ShapeDtypeStruct((rows, D), BF...]
    reshape x3 -> x0, local copies, waits for them, and re-layouts: 3.41 us -> none  [fast_shards(): array.reshape(1, size)]
    pallas_call x3 -> x0, other arithmetic: 2.06 us -> none  [adam_in(): pl.pallas_call(adam_in_kernel, grid=(rows // ADAM_ROWS,), in_specs=[pl.Bl...]
where the time goes in v2:
time: 178 us; the launch traced here: 177 us
  Pallas kernels  168 us (94%)
  local copies, waits for them, and re-layouts  7.95 us (4%)
    pallas_call x1, Pallas kernels, back(): pl.pallas_call(back_kernel, out_shape=(jax.ShapeDtypeStruct((rows, D), BF...  93.4 us
    pallas_call x1, Pallas kernels, front(): pl.pallas_call(front_kernel, out_shape=(jax.ShapeDtypeStruct((4 * in_mast...  59.4 us
    pallas_call x1, Pallas kernels, adam(): pl.pallas_call(adam_kernel, out_shape=shapes(in_arrays[0], True) + shapes...  15.1 us
    unnamed x20, local copies, waits for them, and re-layouts  7.95 us

profile of v2, /device:TPU:0, one launch (start us, length us, event | category | flops | bytes accessed | tf_op | source)
XLA Modules:
  0.0 177.4 jit_solution(511528264709115515)
XLA Ops:
  1.3 0.1 multiply_sine_fusion
  1.5 0.0 copy-start
  1.5 1.9 %copy-done = f32[192,3968]{1,0:T(8,128)S(1)} copy-done((f32[192,3968]{1,0:T(8,128)S(1)}, f32[192,3968]{1,0:T(8,128)}, u32[]{:S(2)}) %copy-start) | copy-done | bytes 3047448
  3.3 0.0 copy-start.1
  3.3 1.8 %copy-done.1 = f32[960,768]{1,0:T(8,128)S(1)} copy-done((f32[960,768]{1,0:T(8,128)S(1)}, f32[960,768]{1,0:T(8,128)}, u32[]{:S(2)}) %copy-start.1) | copy-done | bytes 2949144
  5.2 0.0 copy-start.3
  5.2 1.0 copy-done.3
  6.2 0.0 copy-start.4
  6.2 1.0 copy-done.4
  7.2 0.0 copy-start.5
  7.2 0.8 copy-done.5
  7.9 0.0 copy-start.6
  7.9 59.4 %front.1 = (bf16[768,2048]{1,0:T(8,128)(2,1)S(1)}, bf16[1920,768]{1,0:T(8,128)(2,1)S(1)}, bf16[2,256,768]{2,1,0:T(8,128)(2,1)S(1)}, bf16[2,256,768]{2,1,0:T(8,12...) custom-call(f32[192,3968]{1,0:T(8,128)S(1)} %copy-done, ...), custom_call_target="tpu_custom_call" | custom-call | tf_op jit(solution)/shard_map/front/pallas_call | solution.py:857
  67.3 0.0 copy-done.6
  67.3 0.0 copy-start.2
  67.3 0.0 copy-start.7
  67.3 0.0 copy-start.8
  67.4 93.4 %back.1 = (bf16[256,768]{1,0:T(8,128)(2,1)S(1)}, bf16[256,768]{1,0:T(8,128)(2,1)S(1)}, bf16[2,4,48,2048]{3,2,1,0:T(8,128)(2,1)S(1)}, bf16[2,4,120,768]{3,2,1,0:T(8,128)(2,1)S(1)}, f32[8,1280]{1,0:T(8,128)S(1)}) custom-call(bf16[768,2048]{1,0:T(8,128)(2,1)S(1)} %get-tuple-element.38.full_in, bf16[1920,768]{1,0:T(8,128)(2,1)S(1)} %get-tuple-element.39.full_out, ...), custom_call_target="tpu_custom_call" | custom-call | tf_op jit(solution)/shard_map/back/pallas_call | solution.py:1338
  160.8 0.0 copy-done.2
  160.8 0.0 copy-done.7
  160.8 0.0 copy-done.8
  160.8 15.1 %adam.1 = (f32[192,3968]{1,0:T(8,128)}, f32[192,3968]{1,0:T(8,128)}, f32[192,3968]{1,0:T(8,128)}, bf16[192,3968]{1,0:T(8,128)(2,1)}, f32[960,768]{1,0:T(8,128)},...) custom-call(bf16[2,192,2048]{2,1,0:T(8,128)(2,1)S(1)} %bitcast.9, ...), custom_call_target="tpu_custom_call" | custom-call | tf_op jit(solution)/shard_map/adam/pallas_call | solution.py:1577
  175.9 0.7 copy.28
  176.7 0.7 copy.29
  (2 shorter events, 0.0 us)
Async XLA Ops:
  1.5 1.9 %copy-start = (f32[192,3968]{1,0:T(8,128)S(1)}, f32[192,3968]{1,0:T(8,128)}, u32[]{:S(2)}) copy-start(f32[192,3968]{1,0:T(8,128)} %in_master.3) | copy-start | bytes 9142276
  3.3 1.8 %copy-start.1 = (f32[960,768]{1,0:T(8,128)S(1)}, f32[960,768]{1,0:T(8,128)}, u32[]{:S(2)}) copy-start(f32[960,768]{1,0:T(8,128)} %out_master.3) | copy-start | bytes 8847364
  5.2 1.0 copy-start.3
  6.2 1.0 copy-start.4
  7.2 0.8 copy-start.5
  7.9 59.4 %copy-start.6 = (f32[7808]{0:T(1024)S(1)}, f32[7808]{0:T(1024)}, u32[]{:S(2)}) copy-start(f32[7808]{0:T(1024)} %param.20) | copy-start | bytes 93700
  67.3 93.4 %copy-start.2 = (f32[960,768]{1,0:T(8,128)S(1)}, f32[960,768]{1,0:T(8,128)}, u32[]{:S(2)}) copy-start(f32[960,768]{1,0:T(8,128)} %out_master.3) | copy-start | bytes 8847364
  67.3 93.4 %copy-start.7 = (f32[7808]{0:T(1024)S(1)}, f32[7808]{0:T(1024)}, u32[]{:S(2)}) copy-start(f32[7808]{0:T(1024)} %param.21) | copy-start | bytes 93700
  67.3 93.4 %copy-start.8 = (f32[7808]{0:T(1024)S(1)}, f32[7808]{0:T(1024)}, u32[]{:S(2)}) copy-start(f32[7808]{0:T(1024)} %param.22) | copy-start | bytes 93700
